TPU v7x, 32 devices: a whole 2x2x4 slice. The times are simulated.
32 devices in a mesh: dp: 2 (over x), expert: 16 (over z, y, core).
Axes of the slice: x: 2, y: 2, z: 4, core: 2. Of those that a mesh axis runs over, the one named last changes fastest.
Arguments:
- tokens: bfloat16 [4096, 1024], P(('dp', 'expert')), may hold values from -6 to 6
- out_grad: bfloat16 [4096, 1024], P(('dp', 'expert')), may hold values from -6 to 6
- expert_ids: int32 [4096, 3], P(('dp', 'expert')), may hold values from 0 to 15, all different within a row; in each aligned block of 128 rows (0 to 127, 128 to 255, ...) at most 30 rows name the same one
- gate_probs: float32 [4096, 3], P(('dp', 'expert')), may hold values from 0.1 to 0.6
- saved_pre: bfloat16 [2, 16, 480, 1536], P('dp', 'expert'), may hold values from -6 to 6
- gate_weight: bfloat16 [16, 1024, 768], P('expert', 'dp'), may hold values from -0.1875 to 0.1875
- up_weight: bfloat16 [16, 1024, 768], P('expert', 'dp'), may hold values from -0.1875 to 0.1875
- down_weight: bfloat16 [16, 1024, 768], P('expert', 'dp'), may hold values from -0.21875 to 0.21875
- basis: bfloat16 [16, 1024, 256], P('expert', 'dp'), may hold values from -0.1875 to 0.1875
Outputs:
- in_grad: bfloat16 [4096, 1024], P(('dp', 'expert'))
- proj_grads: float32 [16, 3, 256, 768], P('expert', None, 'dp')
Inputs may be any that keep to these rules, and one draw needn't show every extreme that they name: `expert_ids`: each token names 3 different experts. The rows of one device name one expert at most 30 times, and on some devices some expert exactly 30 times.
All inputs are finite; a program needn't handle non-finite values.
Results may differ from a plain program's by a relative error of at most 0.0091.
Values may be sent and summed in bfloat16 or wider, within the bound.
A program may use at most 64 MiB of HBM per device.

v0:
```python
import functools
import jax
import jax.numpy as jnp
from jax import lax
from jax.experimental import pallas as pl
from jax.experimental.pallas import tpu as pltpu
from jax.sharding import PartitionSpec as P

MESH = pl.DeviceIdType.MESH
F32 = jnp.float32
BF16 = jnp.bfloat16


def dot(left, right, dims):
    return lax.dot_general(left, right, (dims, ((), ())), preferred_element_type=F32)


NN = ((1,), (0,))
TN = ((0,), (0,))
NT = ((1,), (1,))


def kernel(
    n_dp, n_ex, cap, cp, cw,
    ids, probs, tok_h, og_h, pre_h, gw, uw, dw, bs,
    in_h, own_ref, prec,
    in_v, tok, og, sx, sg, rx, rg, dfull, bfull, gfull, ufull, pre, act_a, act_b, hid, ggrad, ugrad,
    rs, rr, terms, psend,
    local_sem, dy_s, dy_r, x_s, x_r, down_s, down_r, base_s, base_r,
    gate_s, gate_r, up_s, up_r, ret_s, ret_r, proj_s, proj_r, in_s,
):
    my_dp = lax.axis_index("dp")
    me = lax.axis_index("expert")
    rows = n_ex * cp
    tokens, width = tok.shape
    topk = ids.shape[0]
    slots, hidden2 = pre.shape
    hidden = hidden2 // 2
    part = width // n_dp
    nc = part // cw
    rank = bfull.shape[1]
    rk = rank // n_dp
    shift = cp.bit_length() - 1

    def block(owner):
        return pl.ds(pl.multiple_of(owner * cp, cp), cp)

    def wpart(owner):
        return pl.ds(pl.multiple_of(owner * part, part), part)

    def ex_peer(k):
        return lax.rem(me + k, n_ex)

    def ex_from(k):
        return lax.rem(me + n_ex - k, n_ex)

    def dp_peer(i):
        return lax.rem(my_dp + i, n_dp)

    def dp_from(i):
        return lax.rem(my_dp + n_dp - i, n_dp)

    barrier = pltpu.get_barrier_semaphore()

    @pl.loop(1, n_ex)
    def _(k):
        pl.semaphore_signal(barrier, inc=1, device_id={"expert": ex_peer(k)}, device_id_type=MESH)

    for i in range(1, n_dp):
        pl.semaphore_signal(barrier, inc=1, device_id={"dp": dp_peer(i)}, device_id_type=MESH)

    local = [
        pltpu.make_async_copy(pre_h.at[0, 0], pre, local_sem.at[0]),
        pltpu.make_async_copy(dw.at[0], dfull.at[wpart(my_dp)], local_sem.at[1]),
        pltpu.make_async_copy(bs.at[0], bfull.at[wpart(my_dp)], local_sem.at[2]),
    ]
    local_n = 3 + 2 * nc
    fetch = [
        pltpu.make_async_copy(og_h, og, local_sem.at[local_n]),
        pltpu.make_async_copy(tok_h, tok, local_sem.at[local_n + 1]),
    ]
    for copy in fetch:
        copy.start()
    for c in range(nc):
        src = pl.ds(c * cw, cw)
        local.append(
            pltpu.make_async_copy(gw.at[0, src], gfull.at[my_dp * nc + c], local_sem.at[3 + 2 * c])
        )
        local.append(
            pltpu.make_async_copy(uw.at[0, src], ufull.at[my_dp * nc + c], local_sem.at[4 + 2 * c])
        )
    for copy in local:
        copy.start()

    line = lax.broadcasted_iota(jnp.int32, (rows, tokens), 0)
    line_expert = lax.shift_right_logical(line, shift)
    line_slot = lax.bitwise_and(line, cp - 1)
    names = [ids[k : k + 1, :] == line_expert for k in range(topk)]
    any_name = functools.reduce(jnp.logical_or, names)
    one, zero = jnp.ones((), F32), jnp.zeros((), F32)
    named = jnp.where(any_name, one, zero).astype(BF16)
    earlier = lax.broadcasted_iota(jnp.int32, (tokens, tokens), 0) < lax.broadcasted_iota(
        jnp.int32, (tokens, tokens), 1
    )
    before = dot(named, jnp.where(earlier, one, zero).astype(BF16), NN)
    at_slot = before == line_slot.astype(F32)
    pick = jnp.where(jnp.logical_and(any_name, at_slot), one, zero).astype(BF16)
    weights = functools.reduce(
        jnp.add, [jnp.where(name, probs[k : k + 1, :], zero) for k, name in enumerate(names)]
    )
    weight = jnp.sum(jnp.where(at_slot, weights, zero), axis=1, keepdims=True)
    fetch[0].wait()
    sg[...] = (dot(pick, og[...], NN) * weight).astype(BF16)

    pl.semaphore_wait(barrier, n_ex - 1 + n_dp - 1)

    def down_copy(i, owner, peer):
        return pltpu.make_async_remote_copy(
            dw.at[0], dfull.at[wpart(owner)], down_s.at[i], down_r.at[i],
            device_id={"dp": peer}, device_id_type=MESH,
        )

    def base_copy(i, owner, peer):
        return pltpu.make_async_remote_copy(
            bs.at[0], bfull.at[wpart(owner)], base_s.at[i], base_r.at[i],
            device_id={"dp": peer}, device_id_type=MESH,
        )

    def gate_copy(i, c, owner, peer):
        return pltpu.make_async_remote_copy(
            gw.at[0, pl.ds(c * cw, cw)], gfull.at[owner * nc + c], gate_s.at[i, c], gate_r.at[i, c],
            device_id={"dp": peer}, device_id_type=MESH,
        )

    def up_copy(i, c, owner, peer):
        return pltpu.make_async_remote_copy(
            uw.at[0, pl.ds(c * cw, cw)], ufull.at[owner * nc + c], up_s.at[i, c], up_r.at[i, c],
            device_id={"dp": peer}, device_id_type=MESH,
        )

    def row_copy(src, dst, send, recv, k, peer, owner):
        return pltpu.make_async_remote_copy(
            src.at[block(peer)], dst.at[block(owner)], send.at[k], recv.at[k],
            device_id={"expert": peer}, device_id_type=MESH,
        )

    def ret_copy(n, j, k, peer, owner):
        return pltpu.make_async_remote_copy(
            rs.at[j, block(peer)], rr.at[j, block(owner)], ret_s.at[n, k], ret_r.at[n, k],
            device_id={"expert": peer}, device_id_type=MESH,
        )

    def proj_copy(i, peer):
        return pltpu.make_async_remote_copy(
            psend.at[i - 1], prec.at[i - 1], proj_s.at[i], proj_r.at[i],
            device_id={"dp": peer}, device_id_type=MESH,
        )

    for i in range(1, n_dp):
        down_copy(i, my_dp, dp_peer(i)).start()

    @pl.loop(1, n_ex)
    def _(k):
        row_copy(sg, rg, dy_s, dy_r, k, ex_peer(k), me).start()

    for i in range(1, n_dp):
        base_copy(i, my_dp, dp_peer(i)).start()
    for i in range(1, n_dp):
        for c in range(nc):
            gate_copy(i, c, my_dp, dp_peer(i)).start()
            up_copy(i, c, my_dp, dp_peer(i)).start()

    fetch[1].wait()
    sx[...] = dot(pick, tok[...], NN).astype(BF16)

    @pl.loop(1, n_ex)
    def _(k):
        row_copy(sx, rx, x_s, x_r, k, ex_peer(k), me).start()

    rg[block(me), :] = sg[block(me), :]
    rx[block(me), :] = sx[block(me), :]

    local[0].wait()
    row = lax.broadcasted_iota(jnp.int32, (rows, slots), 0)
    inner = lax.bitwise_and(row, cp - 1)
    source = lax.shift_right_logical(row, shift) * cap + inner
    spread_mask = jnp.logical_and(
        source == lax.broadcasted_iota(jnp.int32, (rows, slots), 1), inner < cap
    )
    spread = jnp.where(spread_mask, one, zero).astype(BF16)
    fw = 256
    for f in range(0, hidden, fw):
        cols = slice(f, f + fw)
        g = dot(spread, pre[:, f : f + fw], NN)
        u = dot(spread, pre[:, hidden + f : hidden + f + fw], NN)
        sig = jax.nn.sigmoid(g)
        gs = g * sig
        act_a[:, cols] = gs
        hid[:, cols] = (gs * u).astype(BF16)
        act_b[:, cols] = u * sig * (1.0 + g * (1.0 - sig))

    local[1].wait()

    @pl.loop(1, n_ex)
    def _(k):
        row_copy(sg, rg, dy_s, dy_r, k, ex_from(k), ex_from(k)).wait_recv()

    for i in range(1, n_dp):
        down_copy(i, dp_from(i), dp_peer(i)).wait_recv()
    for f in range(0, hidden, fw):
        cols = slice(f, f + fw)
        hg = dot(rg[...], dfull[:, cols], NN)
        ugrad[:, cols] = (hg * act_a[:, cols]).astype(BF16)
        ggrad[:, cols] = (hg * act_b[:, cols]).astype(BF16)

    def row_grad(n, j):
        out = dot(ggrad[...], gfull[j], NT) + dot(ugrad[...], ufull[j], NT)
        rs[j] = out.astype(BF16)

        @pl.loop(1, n_ex)
        def _(k):
            ret_copy(n, j, k, ex_peer(k), me).start()

        rr[j, block(me), :] = rs[j, block(me), :]

    stored = []

    def combine(n, j):
        @pl.loop(1, n_ex)
        def _(k):
            ret_copy(n, j, k, ex_from(k), ex_from(k)).wait_recv()

        cols = pl.ds(pl.multiple_of(j * cw, cw), cw)
        in_v[j] = dot(pick, rr[j], TN).astype(BF16)
        stored.append(pltpu.make_async_copy(in_v.at[j], in_h.at[:, cols], in_s.at[n]))
        stored[-1].start()

    for c in range(nc):
        local[3 + 2 * c].wait()
        local[4 + 2 * c].wait()
        row_grad(c, my_dp * nc + c)

    local[2].wait()
    for i in range(1, n_dp):
        base_copy(i, dp_from(i), dp_peer(i)).wait_recv()
    dy_proj = dot(rg[...], bfull[...], NN).astype(BF16)
    terms[2] = dot(dy_proj, hid[...], TN)

    @pl.loop(1, n_ex)
    def _(k):
        row_copy(sx, rx, x_s, x_r, k, ex_from(k), ex_from(k)).wait_recv()

    x_proj = dot(rx[...], bfull[...], NN).astype(BF16)
    terms[0] = dot(x_proj, ggrad[...], TN)
    terms[1] = dot(x_proj, ugrad[...], TN)
    for i in range(1, n_dp):
        theirs = pl.ds(pl.multiple_of(dp_peer(i) * rk, rk), rk)
        psend[i - 1] = terms[:, theirs, :].astype(BF16)
        proj_copy(i, dp_peer(i)).start()
    mine = pl.ds(pl.multiple_of(my_dp * rk, rk), rk)
    own_copy = pltpu.make_async_copy(
        terms.at[:, mine, :], own_ref, local_sem.at[local_n + 2]
    )
    own_copy.start()

    for c in range(nc):
        combine(c, my_dp * nc + c)

    order = [(i, c) for i in range(1, n_dp) for c in range(nc)]
    for n, (i, c) in enumerate(order):
        gate_copy(i, c, dp_from(i), dp_peer(i)).wait_recv()
        up_copy(i, c, dp_from(i), dp_peer(i)).wait_recv()
        row_grad(nc + n, dp_from(i) * nc + c)
        if n:
            last_i, last_c = order[n - 1]
            combine(nc + n - 1, dp_from(last_i) * nc + last_c)
    last_i, last_c = order[-1]
    combine(nc + len(order) - 1, dp_from(last_i) * nc + last_c)

    for i in range(1, n_dp):
        down_copy(i, my_dp, dp_peer(i)).wait_send()
        base_copy(i, my_dp, dp_peer(i)).wait_send()
        for c in range(nc):
            gate_copy(i, c, my_dp, dp_peer(i)).wait_send()
            up_copy(i, c, my_dp, dp_peer(i)).wait_send()

    @pl.loop(1, n_ex)
    def _(k):
        row_copy(sg, rg, dy_s, dy_r, k, ex_peer(k), me).wait_send()
        row_copy(sx, rx, x_s, x_r, k, ex_peer(k), me).wait_send()

    spots = [my_dp * nc + c for c in range(nc)] + [dp_from(i) * nc + c for i, c in order]
    for n, j in enumerate(spots):

        @pl.loop(1, n_ex)
        def _(k, n=n, j=j):
            ret_copy(n, j, k, ex_peer(k), me).wait_send()

    for copy in stored:
        copy.wait()
    own_copy.wait()
    for i in range(1, n_dp):
        proj_copy(i, dp_peer(i)).wait_recv()
        proj_copy(i, dp_peer(i)).wait_send()


def finish(n_peers, in_h, own_h, prec_h, in_ref, proj_ref, rows, own, prec, total, in_s, own_s, prec_s, out_s):
    loads = []
    for t in range(own.shape[0]):
        pieces = [pltpu.make_async_copy(own_h.at[t], own.at[t], own_s.at[t])]
        for i in range(n_peers):
            pieces.append(
                pltpu.make_async_copy(prec_h.at[i, t], prec.at[i, t], prec_s.at[i, t])
            )
        for copy in pieces:
            copy.start()
        loads.append(pieces)
    load = pltpu.make_async_copy(in_h, rows, in_s.at[0])
    load.start()
    stores = []
    for t, pieces in enumerate(loads):
        for copy in pieces:
            copy.wait()
        value = own[t]
        for i in range(n_peers):
            value = value + prec[i, t].astype(F32)
        total[t] = value
        stores.append(pltpu.make_async_copy(total.at[t], proj_ref.at[0, t], out_s.at[t]))
        stores[-1].start()
    load.wait()
    stores.append(pltpu.make_async_copy(rows, in_ref, in_s.at[1]))
    stores[-1].start()
    for copy in stores:
        copy.wait()


def body(
    tokens, out_grad, expert_ids, gate_probs, saved_pre, gate_weight, up_weight, down_weight, basis
):
    n_dp, n_ex = lax.axis_size("dp"), lax.axis_size("expert")
    tok_rows, width = tokens.shape
    slots, hidden2 = saved_pre.shape[2:]
    hidden = hidden2 // 2
    cap = slots // n_ex
    cp = max(16, 1 << (cap - 1).bit_length())
    rows = n_ex * cp
    part = gate_weight.shape[1]
    cw = min(256, part)
    nc = part // cw
    chunks = width // cw
    rank = basis.shape[2]
    rk = rank // n_dp
    vmem = pl.BlockSpec(memory_space=pltpu.VMEM)
    hbm = pl.BlockSpec(memory_space=pl.ANY)
    dma = pltpu.SemaphoreType.DMA
    scratch = [
        pltpu.VMEM((chunks, tok_rows, cw), BF16),
        pltpu.VMEM((tok_rows, width), BF16),
        pltpu.VMEM((tok_rows, width), BF16),
        pltpu.VMEM((rows, width), BF16),
        pltpu.VMEM((rows, width), BF16),
        pltpu.VMEM((rows, width), BF16),
        pltpu.VMEM((rows, width), BF16),
        pltpu.VMEM((width, hidden), BF16),
        pltpu.VMEM((width, rank), BF16),
        pltpu.VMEM((chunks, cw, hidden), BF16),
        pltpu.VMEM((chunks, cw, hidden), BF16),
        pltpu.VMEM((slots, hidden2), BF16),
        pltpu.VMEM((rows, hidden), F32),
        pltpu.VMEM((rows, hidden), F32),
        pltpu.VMEM((rows, hidden), BF16),
        pltpu.VMEM((rows, hidden), BF16),
        pltpu.VMEM((rows, hidden), BF16),
        pltpu.VMEM((chunks, rows, cw), BF16),
        pltpu.VMEM((chunks, rows, cw), BF16),
        pltpu.VMEM((3, rank, hidden), F32),
        pltpu.VMEM((n_dp - 1, 3, rk, hidden), BF16),
        dma((6 + 2 * nc,)),
        dma((n_ex,)), dma((n_ex,)), dma((n_ex,)), dma((n_ex,)),
        dma((n_dp,)), dma((n_dp,)), dma((n_dp,)), dma((n_dp,)),
        dma((n_dp, nc)), dma((n_dp, nc)), dma((n_dp, nc)), dma((n_dp, nc)),
        dma((chunks, n_ex)), dma((chunks, n_ex)),
        dma((n_dp,)), dma((n_dp,)), dma((chunks,)),
    ]
    in_part, own, received = pl.pallas_call(
        functools.partial(kernel, n_dp, n_ex, cap, cp, cw),
        out_shape=(
            jax.ShapeDtypeStruct((tok_rows, width), BF16),
            jax.ShapeDtypeStruct((3, rk, hidden), F32),
            jax.ShapeDtypeStruct((n_dp - 1, 3, rk, hidden), BF16),
        ),
        in_specs=[vmem] * 2 + [hbm] * 7,
        out_specs=(hbm, hbm, hbm),
        scratch_shapes=scratch,
        compiler_params=pltpu.CompilerParams(
            collective_id=0, has_side_effects=True, vmem_limit_bytes=60 * 1024 * 1024
        ),
    )(
        expert_ids.T, gate_probs.T, tokens, out_grad, saved_pre,
        gate_weight, up_weight, down_weight, basis,
    )
    return pl.pallas_call(
        functools.partial(finish, n_dp - 1),
        out_shape=(
            jax.ShapeDtypeStruct((tok_rows, width), BF16),
            jax.ShapeDtypeStruct((1, 3, rk, hidden), F32),
        ),
        in_specs=[hbm, hbm, hbm],
        out_specs=(hbm, hbm),
        scratch_shapes=[
            pltpu.VMEM((tok_rows, width), BF16),
            pltpu.VMEM((3, rk, hidden), F32),
            pltpu.VMEM((n_dp - 1, 3, rk, hidden), BF16),
            pltpu.VMEM((3, rk, hidden), F32),
            dma((2,)), dma((3,)), dma((n_dp - 1, 3)), dma((3,)),
        ],
    )(in_part, own, received)


def solution(mesh):
    return jax.shard_map(
        body,
        mesh=mesh,
        in_specs=(
            P(("dp", "expert"), None),
            P(("dp", "expert"), None),
            P(("dp", "expert"), None),
            P(("dp", "expert"), None),
            P("dp", "expert", None, None),
            P("expert", "dp", None),
            P("expert", "dp", None),
            P("expert", "dp", None),
            P("expert", "dp", None),
        ),
        out_specs=(P(("dp", "expert"), None), P("expert", None, "dp", None)),
        check_vma=False,
    )
```

profile of v0, /device:TPU:0, one launch (start us, length us, event | category | flops | bytes accessed | tf_op | source)
XLA Modules:
  0.0 83.5 jit_solution(4506082969903162525)
XLA Ops:
  0.6 80.4 %shard_map.104 = (bf16[128,1024]{1,0:T(8,128)(2,1)}, f32[3,128,768]{2,1,0:T(8,128)}, bf16[1,3,128,768]{3,2,1,0:T(8,128)(2,1)}) custom-call(s32[3,128]{1,0:T(4,128)} %bitcast.2, f32[3,128]{1,0:T(4,128)} %bitcast.3, bf16[128,1024]{1,0:T(8,128)(2,1)} %tok_h.1, bf16[128,1024]{1,0:T(8,128)(2,1)} %og_h.1, bf16[1,1,480,1536]{3,2,1,0:T(8,128)(2,1)} %pre_h.1, ...), custom_call_target="tpu_custom_call" | custom-call | tf_op jit(solution)/shard_map/pallas_call | solution.py:385
  81.1 2.4 %shard_map.105 = (bf16[128,1024]{1,0:T(8,128)(2,1)}, f32[1,3,128,768]{3,2,1,0:T(8,128)}) custom-call(bf16[128,1024]{1,0:T(8,128)(2,1)} %get-tuple-element.5.in_h, f32[3,128,768]{2,1,0:T(8,128)} %get-tuple-element.6.own_h, bf16[1,3,128,768]{3,2,1,0:T(8,128)(2,1)} %get-tuple-element.7.prec_h), custom_call_target="tpu_custom_call" | custom-call | tf_op jit(solution)/shard_map/pallas_call | solution.py:402
where the time goes:
time: 83.7 us; the launch traced here: 83.5 us
  Pallas kernels  82.8 us (99%)
    pallas_call x1, Pallas kernels, body(): pl.pallas_call(functools.partial(kernel, n_dp, n_ex, cap, cp, cw), out_sh...  80.4 us
    pallas_call x1, Pallas kernels, body(): pl.pallas_call(functools.partial(finish, n_dp - 1), out_shape=(jax.ShapeD...  2.4 us

commit v1 on v0

v1 whole, which is shorter than its diff:
```python
import functools
import jax
import jax.numpy as jnp
from jax import lax
from jax.experimental import pallas as pl
from jax.experimental.pallas import tpu as pltpu
from jax.sharding import PartitionSpec as P

MESH = pl.DeviceIdType.MESH
F32 = jnp.float32
BF16 = jnp.bfloat16
LEVELS = 4


def dot(left, right, dims):
    return lax.dot_general(left, right, (dims, ((), ())), preferred_element_type=F32)


NN = ((1,), (0,))
TN = ((0,), (0,))
NT = ((1,), (1,))


def kernel(
    n_dp, n_ex, cap, cp,
    ids, probs, tok_h, og_h, pre_h, gw_h, uw_h, dw, bs,
    in_h, proj_h,
    tok, og, tok2, ids2, idsd, pick_v, sx, sg, rx, rg, dyc, spr, dfull, bfull, gw, uw, pre,
    act_a, act_b, hid, gu, px, pdy, rs, rr, in_v, psend, prec, term, total,
    local_sem, pre_sem, dy_s, dy_r, x_s, x_r, relay_s, relay_r, down_s, down_r, base_s, base_r,
    gu_s, gu_r, ret_s, ret_r, px_s, px_r, proj_s, proj_r, in_s, in_r, ids_s, ids_r, out_s,
):
    my_dp = lax.axis_index("dp")
    me = lax.axis_index("expert")
    rows = n_ex * cp
    half = n_ex // 2
    nl = n_ex // LEVELS
    lrows = nl * cp
    lcap = nl * cap
    tokens, width = tok.shape
    topk = ids.shape[0]
    hidden = dfull.shape[1]
    part = width // n_dp
    rank = bfull.shape[1]
    rk = rank // n_dp
    shift = cp.bit_length() - 1
    fw = 256

    z = lax.div(me, nl)
    spot = lax.rem(me, nl)
    mate = lax.rem(me + half, n_ex)
    half0 = lax.div(me, half) * half
    levels = [z + 1 - 2 * lax.rem(z, 2), lax.rem(z + 2, LEVELS), LEVELS - 1 - z, z]
    own = LEVELS - 1

    def block(owner):
        return pl.ds(pl.multiple_of(owner * cp, cp), cp)

    def wpart(owner):
        return pl.ds(pl.multiple_of(owner * part, part), part)

    def rpart(owner):
        return pl.ds(pl.multiple_of(owner * rk, rk), rk)

    def rank_cols(owner):
        line = lax.broadcasted_iota(jnp.int32, (rank, rk), 0)
        lane = lax.broadcasted_iota(jnp.int32, (rank, rk), 1) + owner * rk
        return jnp.where(line == lane, one, zero).astype(BF16)

    def lpart(j):
        return pl.ds(pl.multiple_of(levels[j] * lrows, lrows), lrows)

    def ex_peer(k):
        return lax.rem(me + k, n_ex)

    def half_peer(k):
        return half0 + lax.rem(me - half0 + k, half)

    def in_level(j, t):
        return levels[j] * nl + lax.rem(spot + t, nl)

    def dp_peer(i):
        return lax.rem(my_dp + i, n_dp)

    def dp_from(i):
        return lax.rem(my_dp + n_dp - i, n_dp)

    pad = gu.shape[3] - lcap
    if pad:
        for j in range(LEVELS):
            pre[j, lcap:, :] = jnp.zeros((pad, 2 * hidden), BF16)
            for i in range(1, n_dp):
                for s in range(2):
                    gu[i, j, s, lcap:, :] = jnp.zeros((pad, hidden), BF16)

    barrier = pltpu.get_barrier_semaphore()

    for i in range(1, n_dp):
        pl.semaphore_signal(barrier, inc=1, device_id={"dp": dp_peer(i)}, device_id_type=MESH)

    @pl.loop(1, n_ex)
    def _(k):
        pl.semaphore_signal(barrier, inc=1, device_id={"expert": ex_peer(k)}, device_id_type=MESH)

    local = [
        pltpu.make_async_copy(og_h, og, local_sem.at[0]),
        pltpu.make_async_copy(tok_h, tok, local_sem.at[1]),
        pltpu.make_async_copy(dw.at[0], dfull.at[wpart(my_dp)], local_sem.at[2]),
        pltpu.make_async_copy(bs.at[0], bfull.at[wpart(my_dp)], local_sem.at[3]),
        pltpu.make_async_copy(gw_h.at[0], gw, local_sem.at[4]),
        pltpu.make_async_copy(uw_h.at[0], uw, local_sem.at[5]),
    ]
    pre_copy = []
    for j in range(LEVELS):
        src = pl.ds(pl.multiple_of(levels[j] * lcap, 8), lcap)
        pre_copy.append(
            pltpu.make_async_copy(pre_h.at[0, 0, src], pre.at[j, pl.ds(0, lcap)], pre_sem.at[j])
        )
    for copy in local[:2] + pre_copy + local[2:]:
        copy.start()

    one, zero = jnp.ones((), F32), jnp.zeros((), F32)
    earlier = lax.broadcasted_iota(jnp.int32, (tokens, tokens), 0) < lax.broadcasted_iota(
        jnp.int32, (tokens, tokens), 1
    )
    earlier = jnp.where(earlier, one, zero).astype(BF16)

    def pick_of(names_of, first, count):
        line = lax.broadcasted_iota(jnp.int32, (count, tokens), 0)
        line_expert = lax.shift_right_logical(line, shift) + first
        line_slot = lax.bitwise_and(line, cp - 1)
        names = [names_of[k : k + 1, :] == line_expert for k in range(topk)]
        any_name = functools.reduce(jnp.logical_or, names)
        named = jnp.where(any_name, one, zero).astype(BF16)
        before = dot(named, earlier, NN)
        at_slot = before == line_slot.astype(F32)
        pick = jnp.where(jnp.logical_and(any_name, at_slot), one, zero).astype(BF16)
        return pick, names, at_slot

    pick, names, at_slot = pick_of(ids, 0, rows)
    pick_v[0] = pick
    weights = functools.reduce(
        jnp.add, [jnp.where(name, probs[k : k + 1, :], zero) for k, name in enumerate(names)]
    )
    weight = jnp.sum(jnp.where(at_slot, weights, zero), axis=1, keepdims=True)

    pl.semaphore_wait(barrier, n_ex - 1 + n_dp - 1)

    def down_copy(i, owner, peer):
        return pltpu.make_async_remote_copy(
            dw.at[0], dfull.at[wpart(owner)], down_s.at[i], down_r.at[i],
            device_id={"dp": peer}, device_id_type=MESH,
        )

    def base_copy(i, owner, peer):
        return pltpu.make_async_remote_copy(
            bs.at[0], bfull.at[wpart(owner)], base_s.at[i], base_r.at[i],
            device_id={"dp": peer}, device_id_type=MESH,
        )

    def ids_copy(i, peer):
        return pltpu.make_async_remote_copy(
            ids, idsd.at[i - 1], ids_s.at[i], ids_r.at[i],
            device_id={"dp": peer}, device_id_type=MESH,
        )

    def mate_ids():
        return pltpu.make_async_remote_copy(
            ids, ids2, ids_s.at[0], ids_r.at[0], device_id={"expert": mate}, device_id_type=MESH
        )

    def mate_tok():
        return pltpu.make_async_remote_copy(
            tok, tok2, relay_s, relay_r, device_id={"expert": mate}, device_id_type=MESH
        )

    def dy_copy(peer, owner):
        return pltpu.make_async_remote_copy(
            sg.at[block(peer)], rg.at[block(owner)], dy_s.at[peer], dy_r.at[owner],
            device_id={"expert": peer}, device_id_type=MESH,
        )

    def x_copy(m, peer, owner):
        return pltpu.make_async_remote_copy(
            sx.at[m, block(peer - half0)], rx.at[block(owner)], x_s.at[m, peer - half0], x_r.at[owner],
            device_id={"expert": peer}, device_id_type=MESH,
        )

    def gu_copy(i, j, peer):
        used = pl.ds(0, lcap)
        return pltpu.make_async_remote_copy(
            gu.at[0, j, :, used], gu.at[i, j, :, used], gu_s.at[i, j], gu_r.at[i, j],
            device_id={"dp": peer}, device_id_type=MESH,
        )

    def px_copy(i, peer):
        return pltpu.make_async_remote_copy(
            px.at[i - 1], px.at[n_dp - 1 + i], px_s.at[i], px_r.at[i],
            device_id={"dp": peer}, device_id_type=MESH,
        )

    def ret_copy(i, j, peer, owner):
        return pltpu.make_async_remote_copy(
            rs.at[i, j, block(lax.rem(peer, nl))], rr.at[i, block(owner)],
            ret_s.at[i, peer], ret_r.at[i, owner],
            device_id={"expert": peer}, device_id_type=MESH,
        )

    def proj_copy(i, peer):
        return pltpu.make_async_remote_copy(
            psend.at[i - 1], prec.at[i - 1], proj_s.at[i], proj_r.at[i],
            device_id={"dp": peer}, device_id_type=MESH,
        )

    def in_copy(i, owner, peer):
        return pltpu.make_async_remote_copy(
            in_v.at[i], in_h.at[:, wpart(owner)], in_s.at[i], in_r.at[i],
            device_id={"dp": peer}, device_id_type=MESH,
        )

    for i in range(1, n_dp):
        down_copy(i, my_dp, dp_peer(i)).start()
    for i in range(1, n_dp):
        base_copy(i, my_dp, dp_peer(i)).start()
    mate_ids().start()
    for i in range(1, n_dp):
        ids_copy(i, dp_peer(i)).start()

    local[0].wait()
    sg[...] = (dot(pick, og[...], NN) * weight).astype(BF16)
    for j in range(LEVELS):

        @pl.loop(int(j == own), nl)
        def _(t, j=j):
            dy_copy(in_level(j, t), me).start()

    rg[block(me), :] = sg[block(me), :]

    local[1].wait()
    mate_tok().start()
    half_rows = pl.ds(pl.multiple_of(half0 * cp, cp), half * cp)
    sx[0] = dot(pick_v[0, half_rows], tok[...], NN).astype(BF16)

    @pl.loop(1, half)
    def _(k):
        x_copy(0, half_peer(k), me).start()

    rx[block(me), :] = sx[0, block(me - half0), :]

    grid = (gu.shape[3], lrows)
    line = lax.broadcasted_iota(jnp.int32, grid, 1)
    inner = lax.bitwise_and(line, cp - 1)
    target = lax.shift_right_logical(line, shift) * cap + inner
    spread = jnp.logical_and(target == lax.broadcasted_iota(jnp.int32, grid, 0), inner < cap)
    spr[...] = jnp.where(spread, one, zero).astype(BF16)

    for j in range(LEVELS):
        pre_copy[j].wait()
        for f in range(0, hidden, fw):
            cols = slice(f, f + fw)
            g = pre[j, :, f : f + fw].astype(F32)
            u = pre[j, :, hidden + f : hidden + f + fw].astype(F32)
            sig = jax.nn.sigmoid(g)
            gs = g * sig
            act_a[j, :, cols] = gs
            hid[j, :, cols] = (gs * u).astype(BF16)
            act_b[j, :, cols] = u * sig * (1.0 + g * (1.0 - sig))

    def row_grad(i, j):
        out = dot(gu[i, j, 0], gw[...], NT) + dot(gu[i, j, 1], uw[...], NT)
        rs[i, j] = dot(spr[...], out.astype(BF16), TN).astype(BF16)

        @pl.loop(int(j == own), nl)
        def _(t):
            ret_copy(i, j, in_level(j, t), me).start()

        if j == own:
            rr[i, block(me), :] = rs[i, j, block(spot), :]

    local[2].wait()
    for i in range(1, n_dp):
        down_copy(i, dp_from(i), dp_peer(i)).wait_recv()

    for j in range(LEVELS):

        @pl.loop(int(j == own), nl)
        def _(t, j=j):
            src = in_level(j, t)
            dy_copy(src, src).wait_recv()

        dyc[j] = dot(spr[...], rg[lpart(j), :], NN).astype(BF16)
        for f in range(0, hidden, fw):
            cols = slice(f, f + fw)
            hg = dot(dyc[j], dfull[:, cols], NN)
            gu[0, j, 1, :, cols] = (hg * act_a[j, :, cols]).astype(BF16)
            gu[0, j, 0, :, cols] = (hg * act_b[j, :, cols]).astype(BF16)
        for i in range(1, n_dp):
            gu_copy(i, j, dp_peer(i)).start()
        if j == 0:
            local[4].wait()
            local[5].wait()
        row_grad(0, j)

    local[3].wait()
    for i in range(1, n_dp):
        base_copy(i, dp_from(i), dp_peer(i)).wait_recv()
    for j in range(LEVELS):
        pdy[j] = dot(dyc[j], bfull[...], NN).astype(BF16)

    def project(left, right):
        return functools.reduce(jnp.add, [dot(left(j), right(j), TN) for j in range(LEVELS)])

    term[...] = project(lambda j: pdy[j], lambda j: hid[j])
    for i in range(1, n_dp):
        psend[i - 1] = term[rpart(dp_peer(i)), :].astype(BF16)
        proj_copy(i, dp_peer(i)).start()
    total[2] = term[rpart(my_dp), :]

    mate_ids().wait_recv()
    pick2, _, _ = pick_of(ids2, half0, half * cp)
    mate_tok().wait_recv()
    sx[1] = dot(pick2, tok2[...], NN).astype(BF16)

    @pl.loop(1, half)
    def _(k):
        x_copy(1, half_peer(k), mate).start()

    rx[block(mate), :] = sx[1, block(me - half0), :]

    for i in range(1, n_dp):
        ids_copy(i, dp_peer(i)).wait_recv()
        pick_v[i] = pick_of(idsd.at[i - 1], 0, rows)[0]

    def theirs(j):
        for i in range(1, n_dp):
            gu_copy(i, j, dp_peer(i)).wait_recv()
            row_grad(i, j)

    theirs(0)
    theirs(1)

    @pl.loop(1, n_ex)
    def _(k):
        src = ex_peer(k)

        @pl.when(src != mate)
        def _():
            x_copy(0, half0, src).wait_recv()

    for j in range(LEVELS):
        xj = dot(spr[...], rx[lpart(j), :], NN).astype(BF16)
        if rk % 128:
            xp = dot(xj, bfull[...], NN).astype(BF16)
        for i in range(n_dp):
            if rk % 128:
                pj = dot(xp, rank_cols(dp_peer(i)), NN)
            else:
                pj = dot(xj, bfull[:, rpart(dp_peer(i))], NN)
            px[(i + n_dp - 1) % n_dp, j] = pj.astype(BF16)
    for i in range(1, n_dp):
        px_copy(i, dp_peer(i)).start()

    theirs(2)

    def x_term(s, i):
        left = px.at[n_dp - 1 + i]
        return project(lambda j: left[j], lambda j: gu[i, j, s])

    for s in range(2):
        total[s] = x_term(s, 0)

    stored = []

    def combine(i):
        @pl.loop(1, n_ex)
        def _(k):
            src = ex_peer(k)
            ret_copy(i, 0, src, src).wait_recv()

        in_v[i] = dot(pick_v[i], rr[i], TN).astype(BF16)

    combine(0)
    stored.append(pltpu.make_async_copy(in_v.at[0], in_h.at[:, wpart(my_dp)], out_s.at[3]))
    stored[-1].start()

    for i in range(1, n_dp):
        proj_copy(i, dp_peer(i)).wait_recv()
        total[2] += prec[i - 1].astype(F32)
    stored.append(pltpu.make_async_copy(total.at[2], proj_h.at[2], out_s.at[2]))
    stored[-1].start()

    theirs(3)
    for i in range(1, n_dp):
        px_copy(i, dp_peer(i)).wait_recv()
        for s in range(2):
            total[s] += x_term(s, i)
    for s in range(2):
        stored.append(pltpu.make_async_copy(total.at[s], proj_h.at[s], out_s.at[s]))
        stored[-1].start()
    for i in range(1, n_dp):
        combine(i)
        in_copy(i, my_dp, dp_from(i)).start()

    for i in range(1, n_dp):
        down_copy(i, my_dp, dp_peer(i)).wait_send()
        base_copy(i, my_dp, dp_peer(i)).wait_send()
        ids_copy(i, dp_peer(i)).wait_send()
        px_copy(i, dp_peer(i)).wait_send()
        proj_copy(i, dp_peer(i)).wait_send()
        for j in range(LEVELS):
            gu_copy(i, j, dp_peer(i)).wait_send()
    mate_ids().wait_send()
    mate_tok().wait_send()

    @pl.loop(1, n_ex)
    def _(k):
        dy_copy(ex_peer(k), me).wait_send()

    @pl.loop(1, half)
    def _(k):
        x_copy(0, half_peer(k), me).wait_send()
        x_copy(1, half_peer(k), mate).wait_send()

    for i in range(n_dp):

        @pl.loop(1, n_ex)
        def _(k, i=i):
            ret_copy(i, 0, ex_peer(k), me).wait_send()

    for copy in stored:
        copy.wait()
    for i in range(1, n_dp):
        in_copy(i, my_dp, dp_from(i)).wait_send()
        in_copy(i, dp_peer(i), dp_from(i)).wait_recv()


def finish(in_h, proj_h, in_ref, proj_ref, rows, proj, load_s, store_s):
    n = proj.shape[0]
    loads = [pltpu.make_async_copy(proj_h.at[t], proj.at[t], load_s.at[t]) for t in range(n)]
    loads.append(pltpu.make_async_copy(in_h, rows, load_s.at[n]))
    stores = [
        pltpu.make_async_copy(proj.at[t], proj_ref.at[0, t], store_s.at[t]) for t in range(n)
    ]
    stores.append(pltpu.make_async_copy(rows, in_ref, store_s.at[n]))
    for copy in loads:
        copy.start()
    for load, store in zip(loads, stores):
        load.wait()
        store.start()
    for copy in stores:
        copy.wait()


def body(
    tokens, out_grad, expert_ids, gate_probs, saved_pre, gate_weight, up_weight, down_weight, basis
):
    n_dp, n_ex = lax.axis_size("dp"), lax.axis_size("expert")
    tok_rows, width = tokens.shape
    topk = expert_ids.shape[1]
    slots, hidden2 = saved_pre.shape[2:]
    hidden = hidden2 // 2
    cap = slots // n_ex
    cp = max(16, 1 << (cap - 1).bit_length())
    rows = n_ex * cp
    nl = n_ex // LEVELS
    lrows = nl * cp
    lpad = -(-nl * cap // 16) * 16
    part = gate_weight.shape[1]
    rank = basis.shape[2]
    rk = rank // n_dp
    vmem = pl.BlockSpec(memory_space=pltpu.VMEM)
    hbm = pl.BlockSpec(memory_space=pl.ANY)
    dma = pltpu.SemaphoreType.DMA
    scratch = [
        pltpu.VMEM((tok_rows, width), BF16),
        pltpu.VMEM((tok_rows, width), BF16),
        pltpu.VMEM((tok_rows, width), BF16),
        pltpu.VMEM((topk, tok_rows), jnp.int32),
        pltpu.VMEM((n_dp - 1, topk, tok_rows), jnp.int32),
        pltpu.VMEM((n_dp, rows, tok_rows), BF16),
        pltpu.VMEM((2, rows // 2, width), BF16),
        pltpu.VMEM((rows, width), BF16),
        pltpu.VMEM((rows, width), BF16),
        pltpu.VMEM((rows, width), BF16),
        pltpu.VMEM((LEVELS, lpad, width), BF16),
        pltpu.VMEM((lpad, lrows), BF16),
        pltpu.VMEM((width, hidden), BF16),
        pltpu.VMEM((width, rank), BF16),
        pltpu.VMEM((part, hidden), BF16),
        pltpu.VMEM((part, hidden), BF16),
        pltpu.VMEM((LEVELS, lpad, hidden2), BF16),
        pltpu.VMEM((LEVELS, lpad, hidden), F32),
        pltpu.VMEM((LEVELS, lpad, hidden), F32),
        pltpu.VMEM((LEVELS, lpad, hidden), BF16),
        pltpu.VMEM((n_dp, LEVELS, 2, lpad, hidden), BF16),
        pltpu.VMEM((2 * n_dp - 1, LEVELS, lpad, rk), BF16),
        pltpu.VMEM((LEVELS, lpad, rank), BF16),
        pltpu.VMEM((n_dp, LEVELS, lrows, part), BF16),
        pltpu.VMEM((n_dp, rows, part), BF16),
        pltpu.VMEM((n_dp, tok_rows, part), BF16),
        pltpu.VMEM((n_dp - 1, rk, hidden), BF16),
        pltpu.VMEM((n_dp - 1, rk, hidden), BF16),
        pltpu.VMEM((rank, hidden), F32),
        pltpu.VMEM((3, rk, hidden), F32),
        dma((6,)), dma((LEVELS,)),
        dma((n_ex,)), dma((n_ex,)), dma((2, n_ex // 2)), dma((n_ex,)), dma, dma,
        dma((n_dp,)), dma((n_dp,)), dma((n_dp,)), dma((n_dp,)),
        dma((n_dp, LEVELS)), dma((n_dp, LEVELS)), dma((n_dp, n_ex)), dma((n_dp, n_ex)),
        dma((n_dp,)), dma((n_dp,)), dma((n_dp,)), dma((n_dp,)),
        dma((n_dp,)), dma((n_dp,)), dma((n_dp,)), dma((n_dp,)), dma((4,)),
    ]
    in_part, proj = pl.pallas_call(
        functools.partial(kernel, n_dp, n_ex, cap, cp),
        out_shape=(
            jax.ShapeDtypeStruct((tok_rows, width), BF16),
            jax.ShapeDtypeStruct((3, rk, hidden), F32),
        ),
        in_specs=[vmem] * 2 + [hbm] * 7,
        out_specs=(hbm, hbm),
        scratch_shapes=scratch,
        compiler_params=pltpu.CompilerParams(
            collective_id=0, has_side_effects=True, vmem_limit_bytes=60 * 1024 * 1024
        ),
    )(
        expert_ids.T, gate_probs.T, tokens, out_grad, saved_pre,
        gate_weight, up_weight, down_weight, basis,
    )
    return pl.pallas_call(
        finish,
        out_shape=(
            jax.ShapeDtypeStruct((tok_rows, width), BF16),
            jax.ShapeDtypeStruct((1, 3, rk, hidden), F32),
        ),
        in_specs=[hbm, hbm],
        out_specs=(hbm, hbm),
        scratch_shapes=[
            pltpu.VMEM((tok_rows, width), BF16),
            pltpu.VMEM((3, rk, hidden), F32),
            dma((4,)), dma((4,)),
        ],
    )(in_part, proj)


def solution(mesh):
    return jax.shard_map(
        body,
        mesh=mesh,
        in_specs=(
            P(("dp", "expert"), None),
            P(("dp", "expert"), None),
            P(("dp", "expert"), None),
            P(("dp", "expert"), None),
            P("dp", "expert", None, None),
            P("expert", "dp", None),
            P("expert", "dp", None),
            P("expert", "dp", None),
            P("expert", "dp", None),
        ),
        out_specs=(P(("dp", "expert"), None), P("expert", None, "dp", None)),
        check_vma=False,
    )
```

time: 83.7 us -> 81.2 us (0.970)
  Pallas kernels: 82.8 us -> 80.4 us
    pallas_call x2, Pallas kernels: 82.8 us -> 80.4 us  [the longest x1 78.2 us: body(): pl.pallas_call(functools.partial(kernel, n_dp, n_ex, cap, cp), out_shape=...]
where the time goes in v1:
time: 81.2 us; the launch traced here: 81 us
  Pallas kernels  80.4 us (99%)
    pallas_call x1, Pallas kernels, body(): pl.pallas_call(functools.partial(kernel, n_dp, n_ex, cap, cp), out_shape=...  78.2 us
    pallas_call x1, Pallas kernels, body(): pl.pallas_call(finish, out_shape=(jax.ShapeDtypeStruct((tok_rows, width),...  2.16 us

profile of v1, /device:TPU:0, one launch (start us, length us, event | category | flops | bytes accessed | tf_op | source)
XLA Modules:
  0.0 81.0 jit_solution(11997496808495115190)
XLA Ops:
  0.6 78.2 %shard_map.104 = (bf16[128,1024]{1,0:T(8,128)(2,1)}, f32[3,128,768]{2,1,0:T(8,128)}) custom-call(s32[3,128]{1,0:T(4,128)} %bitcast.2, f32[3,128]{1,0:T(4,128)} %bitcast.3, bf16[128,1024]{1,0:T(8,128)(2,1)} %tok_h.1, bf16[128,1024]{1,0:T(8,128)(2,1)} %og_h.1, bf16[1,1,480,1536]{3,2,1,0:T(8,128)(2,1)} %pre_h.1, bf16[1,512,768]{2,1,0:T(8,128)(2,1)} %gw_h.1, ...), custom_call_target="tpu_custom_call" | custom-call | tf_op jit(solution)/shard_map/pallas_call | solution.py:512
  78.9 2.2 %shard_map.105 = (bf16[128,1024]{1,0:T(8,128)(2,1)}, f32[1,3,128,768]{3,2,1,0:T(8,128)}) custom-call(bf16[128,1024]{1,0:T(8,128)(2,1)} %get-tuple-element.4.in_h, f32[3,128,768]{2,1,0:T(8,128)} %get-tuple-element.5.proj_h), custom_call_target="tpu_custom_call" | custom-call | tf_op jit(solution)/shard_map/pallas_call | solution.py:528

commit v2 on v1

--- a/solution.py
+++ b/solution.py
@@ -23,9 +23,9 @@
 
 def kernel(
     n_dp, n_ex, cap, cp,
-    ids, probs, tok_h, og_h, pre_h, gw_h, uw_h, dw, bs,
+    ids_h, probs_h, tok_h, og_h, pre_h, gw_h, uw_h, dw, bs,
     in_h, proj_h,
-    tok, og, tok2, ids2, idsd, pick_v, sx, sg, rx, rg, dyc, spr, dfull, bfull, gw, uw, pre,
+    ids, probs, tok, og, tok2, ids2, idsd, pick_v, pick_m, sx, sg, rx, rg, dyc, spr, dfull, bfull, gw, uw, pre,
     act_a, act_b, hid, gu, px, pdy, rs, rr, in_v, psend, prec, term, total,
     local_sem, pre_sem, dy_s, dy_r, x_s, x_r, relay_s, relay_r, down_s, down_r, base_s, base_r,
     gu_s, gu_r, ret_s, ret_r, px_s, px_r, proj_s, proj_r, in_s, in_r, ids_s, ids_r, out_s,
@@ -85,6 +85,13 @@
     def dp_from(i):
         return lax.rem(my_dp + n_dp - i, n_dp)
 
+    first = [
+        pltpu.make_async_copy(ids_h, ids, local_sem.at[6]),
+        pltpu.make_async_copy(probs_h, probs, local_sem.at[7]),
+    ]
+    for copy in first:
+        copy.start()
+
     pad = gu.shape[3] - lcap
     if pad:
         for j in range(LEVELS):
@@ -137,6 +144,8 @@
         pick = jnp.where(jnp.logical_and(any_name, at_slot), one, zero).astype(BF16)
         return pick, names, at_slot
 
+    for copy in first:
+        copy.wait()
     pick, names, at_slot = pick_of(ids, 0, rows)
     pick_v[0] = pick
     weights = functools.reduce(
@@ -316,20 +325,12 @@
         proj_copy(i, dp_peer(i)).start()
     total[2] = term[rpart(my_dp), :]
 
+    for i in range(1, n_dp):
+        ids_copy(i, dp_peer(i)).wait_recv()
+        pick_v[i] = pick_of(idsd.at[i - 1], 0, rows)[0]
     mate_ids().wait_recv()
     pick2, _, _ = pick_of(ids2, half0, half * cp)
-    mate_tok().wait_recv()
-    sx[1] = dot(pick2, tok2[...], NN).astype(BF16)
-
-    @pl.loop(1, half)
-    def _(k):
-        x_copy(1, half_peer(k), mate).start()
-
-    rx[block(mate), :] = sx[1, block(me - half0), :]
-
-    for i in range(1, n_dp):
-        ids_copy(i, dp_peer(i)).wait_recv()
-        pick_v[i] = pick_of(idsd.at[i - 1], 0, rows)[0]
+    pick_m[...] = pick2
 
     def theirs(j):
         for i in range(1, n_dp):
@@ -337,6 +338,16 @@
             row_grad(i, j)
 
     theirs(0)
+
+    mate_tok().wait_recv()
+    sx[1] = dot(pick_m[...], tok2[...], NN).astype(BF16)
+
+    @pl.loop(1, half)
+    def _(k):
+        x_copy(1, half_peer(k), mate).start()
+
+    rx[block(mate), :] = sx[1, block(me - half0), :]
+
     theirs(1)
 
     @pl.loop(1, n_ex)
@@ -361,6 +372,7 @@
         px_copy(i, dp_peer(i)).start()
 
     theirs(2)
+    theirs(3)
 
     def x_term(s, i):
         left = px.at[n_dp - 1 + i]
@@ -382,14 +394,15 @@
     combine(0)
     stored.append(pltpu.make_async_copy(in_v.at[0], in_h.at[:, wpart(my_dp)], out_s.at[3]))
     stored[-1].start()
+    for i in range(1, n_dp):
+        combine(i)
+        in_copy(i, my_dp, dp_from(i)).start()
 
     for i in range(1, n_dp):
         proj_copy(i, dp_peer(i)).wait_recv()
         total[2] += prec[i - 1].astype(F32)
     stored.append(pltpu.make_async_copy(total.at[2], proj_h.at[2], out_s.at[2]))
     stored[-1].start()
-
-    theirs(3)
     for i in range(1, n_dp):
         px_copy(i, dp_peer(i)).wait_recv()
         for s in range(2):
@@ -397,9 +410,6 @@
     for s in range(2):
         stored.append(pltpu.make_async_copy(total.at[s], proj_h.at[s], out_s.at[s]))
         stored[-1].start()
-    for i in range(1, n_dp):
-        combine(i)
-        in_copy(i, my_dp, dp_from(i)).start()
 
     for i in range(1, n_dp):
         down_copy(i, my_dp, dp_peer(i)).wait_send()
@@ -468,16 +478,18 @@
     part = gate_weight.shape[1]
     rank = basis.shape[2]
     rk = rank // n_dp
-    vmem = pl.BlockSpec(memory_space=pltpu.VMEM)
     hbm = pl.BlockSpec(memory_space=pl.ANY)
     dma = pltpu.SemaphoreType.DMA
     scratch = [
+        pltpu.VMEM((topk, tok_rows), jnp.int32),
+        pltpu.VMEM((topk, tok_rows), F32),
         pltpu.VMEM((tok_rows, width), BF16),
         pltpu.VMEM((tok_rows, width), BF16),
         pltpu.VMEM((tok_rows, width), BF16),
         pltpu.VMEM((topk, tok_rows), jnp.int32),
         pltpu.VMEM((n_dp - 1, topk, tok_rows), jnp.int32),
         pltpu.VMEM((n_dp, rows, tok_rows), BF16),
+        pltpu.VMEM((rows // 2, tok_rows), BF16),
         pltpu.VMEM((2, rows // 2, width), BF16),
         pltpu.VMEM((rows, width), BF16),
         pltpu.VMEM((rows, width), BF16),
@@ -502,7 +514,7 @@
         pltpu.VMEM((n_dp - 1, rk, hidden), BF16),
         pltpu.VMEM((rank, hidden), F32),
         pltpu.VMEM((3, rk, hidden), F32),
-        dma((6,)), dma((LEVELS,)),
+        dma((8,)), dma((LEVELS,)),
         dma((n_ex,)), dma((n_ex,)), dma((2, n_ex // 2)), dma((n_ex,)), dma, dma,
         dma((n_dp,)), dma((n_dp,)), dma((n_dp,)), dma((n_dp,)),
         dma((n_dp, LEVELS)), dma((n_dp, LEVELS)), dma((n_dp, n_ex)), dma((n_dp, n_ex)),
@@ -515,7 +527,7 @@
             jax.ShapeDtypeStruct((tok_rows, width), BF16),
             jax.ShapeDtypeStruct((3, rk, hidden), F32),
         ),
-        in_specs=[vmem] * 2 + [hbm] * 7,
+        in_specs=[hbm] * 9,
         out_specs=(hbm, hbm),
         scratch_shapes=scratch,
         compiler_params=pltpu.CompilerParams(

time: 81.2 us -> 79.3 us (0.977)
  Pallas kernels: 80.4 us -> 78.5 us
    pallas_call x1, Pallas kernels: 78.2 us -> 76.4 us  [body(): pl.pallas_call(functools.partial(kernel, n_dp, n_ex, cap, cp), out_shape=...]
where the time goes in v2:
time: 79.3 us; the launch traced here: 79.2 us
  Pallas kernels  78.5 us (99%)
    pallas_call x1, Pallas kernels, body(): pl.pallas_call(functools.partial(kernel, n_dp, n_ex, cap, cp), out_shape=...  76.4 us
    pallas_call x1, Pallas kernels, body(): pl.pallas_call(finish, out_shape=(jax.ShapeDtypeStruct((tok_rows, width),...  2.16 us

profile of v2, /device:TPU:0, one launch (start us, length us, event | category | flops | bytes accessed | tf_op | source)
XLA Modules:
  0.0 79.2 jit_solution(6369504935373256462)
XLA Ops:
  0.6 76.4 %shard_map.104 = (bf16[128,1024]{1,0:T(8,128)(2,1)}, f32[3,128,768]{2,1,0:T(8,128)}) custom-call(s32[3,128]{1,0:T(4,128)} %bitcast.2, f32[3,128]{1,0:T(4,128)} %bitcast.3, bf16[128,1024]{1,0:T(8,128)(2,1)} %tok_h.1, bf16[128,1024]{1,0:T(8,128)(2,1)} %og_h.1, bf16[1,1,480,1536]{3,2,1,0:T(8,128)(2,1)} %pre_h.1, bf16[1,512,768]{2,1,0:T(8,128)(2,1)} %gw_h.1, ...), custom_call_target="tpu_custom_call" | custom-call | tf_op jit(solution)/shard_map/pallas_call | solution.py:524
  77.0 2.2 %shard_map.105 = (bf16[128,1024]{1,0:T(8,128)(2,1)}, f32[1,3,128,768]{3,2,1,0:T(8,128)}) custom-call(bf16[128,1024]{1,0:T(8,128)(2,1)} %get-tuple-element.4.in_h, f32[3,128,768]{2,1,0:T(8,128)} %get-tuple-element.5.proj_h), custom_call_target="tpu_custom_call" | custom-call | tf_op jit(solution)/shard_map/pallas_call | solution.py:540

commit v3 on v2

--- a/solution.py
+++ b/solution.py
@@ -25,9 +25,9 @@
     n_dp, n_ex, cap, cp,
     ids_h, probs_h, tok_h, og_h, pre_h, gw_h, uw_h, dw, bs,
     in_h, proj_h,
-    ids, probs, tok, og, tok2, ids2, idsd, pick_v, pick_m, sx, sg, rx, rg, dyc, spr, dfull, bfull, gw, uw, pre,
+    ids, probs, tok, og, tok2, og2, ids2, probs2, idsd, pick_v, sx, sg, rx, rg, dyc, spr, dfull, bfull, gw, uw, pre,
     act_a, act_b, hid, gu, px, pdy, rs, rr, in_v, psend, prec, term, total,
-    local_sem, pre_sem, dy_s, dy_r, x_s, x_r, relay_s, relay_r, down_s, down_r, base_s, base_r,
+    local_sem, pre_sem, dy_s, dy_r, x_s, x_r, mate_s, mate_r, down_s, down_r, base_s, base_r,
     gu_s, gu_r, ret_s, ret_r, px_s, px_r, proj_s, proj_r, in_s, in_r, ids_s, ids_r, out_s,
 ):
     my_dp = lax.axis_index("dp")
@@ -144,14 +144,16 @@
         pick = jnp.where(jnp.logical_and(any_name, at_slot), one, zero).astype(BF16)
         return pick, names, at_slot
 
+    def half_pick(names_of, weights_of):
+        pick, names, at_slot = pick_of(names_of, half0, half * cp)
+        weights = functools.reduce(
+            jnp.add, [jnp.where(name, weights_of[k : k + 1, :], zero) for k, name in enumerate(names)]
+        )
+        return pick, jnp.sum(jnp.where(at_slot, weights, zero), axis=1, keepdims=True)
+
     for copy in first:
         copy.wait()
-    pick, names, at_slot = pick_of(ids, 0, rows)
-    pick_v[0] = pick
-    weights = functools.reduce(
-        jnp.add, [jnp.where(name, probs[k : k + 1, :], zero) for k, name in enumerate(names)]
-    )
-    weight = jnp.sum(jnp.where(at_slot, weights, zero), axis=1, keepdims=True)
+    pick, weight = half_pick(ids, probs)
 
     pl.semaphore_wait(barrier, n_ex - 1 + n_dp - 1)
 
@@ -173,26 +175,28 @@
             device_id={"dp": peer}, device_id_type=MESH,
         )
 
-    def mate_ids():
-        return pltpu.make_async_remote_copy(
-            ids, ids2, ids_s.at[0], ids_r.at[0], device_id={"expert": mate}, device_id_type=MESH
-        )
-
-    def mate_tok():
-        return pltpu.make_async_remote_copy(
-            tok, tok2, relay_s, relay_r, device_id={"expert": mate}, device_id_type=MESH
-        )
-
-    def dy_copy(peer, owner):
-        return pltpu.make_async_remote_copy(
-            sg.at[block(peer)], rg.at[block(owner)], dy_s.at[peer], dy_r.at[owner],
+    def mate_copy(n):
+        src, dst = ((og, og2), (tok, tok2), (ids, ids2), (probs, probs2))[n]
+        return pltpu.make_async_remote_copy(
+            src, dst, mate_s.at[n], mate_r.at[n], device_id={"expert": mate}, device_id_type=MESH
+        )
+
+    def dy_copy(m, peer, owner, j):
+        return pltpu.make_async_remote_copy(
+            sg.at[m, block(peer - half0)], rg.at[block(owner)], dy_s.at[m], dy_r.at[j],
             device_id={"expert": peer}, device_id_type=MESH,
         )
 
     def x_copy(m, peer, owner):
         return pltpu.make_async_remote_copy(
-            sx.at[m, block(peer - half0)], rx.at[block(owner)], x_s.at[m, peer - half0], x_r.at[owner],
+            sx.at[m, block(peer - half0)], rx.at[block(owner)], x_s.at[m], x_r.at[0],
             device_id={"expert": peer}, device_id_type=MESH,
+        )
+
+    def blocks(buffer, count, send, recv):
+        span = buffer.at[pl.ds(0, count * cp)]
+        return pltpu.make_async_remote_copy(
+            span, span, send, recv, device_id={"expert": mate}, device_id_type=MESH
         )
 
     def gu_copy(i, j, peer):
@@ -211,7 +215,7 @@
     def ret_copy(i, j, peer, owner):
         return pltpu.make_async_remote_copy(
             rs.at[i, j, block(lax.rem(peer, nl))], rr.at[i, block(owner)],
-            ret_s.at[i, peer], ret_r.at[i, owner],
+            ret_s.at[i], ret_r.at[i],
             device_id={"expert": peer}, device_id_type=MESH,
         )
 
@@ -229,32 +233,37 @@
 
     for i in range(1, n_dp):
         down_copy(i, my_dp, dp_peer(i)).start()
+    mate_copy(2).start()
+    mate_copy(3).start()
+    local[0].wait()
+    mate_copy(0).start()
     for i in range(1, n_dp):
         base_copy(i, my_dp, dp_peer(i)).start()
-    mate_ids().start()
     for i in range(1, n_dp):
         ids_copy(i, dp_peer(i)).start()
 
-    local[0].wait()
-    sg[...] = (dot(pick, og[...], NN) * weight).astype(BF16)
-    for j in range(LEVELS):
-
-        @pl.loop(int(j == own), nl)
-        def _(t, j=j):
-            dy_copy(in_level(j, t), me).start()
-
-    rg[block(me), :] = sg[block(me), :]
-
+    def dispatch_dy(m, owner):
+        for near, tag in ((0, 0 if m == 0 else 2), (own, own if m == 0 else 1)):
+
+            @pl.loop(int(near == own), nl)
+            def _(t):
+                dy_copy(m, in_level(near, t), owner, tag).start()
+
+        rg[block(owner), :] = sg[m, block(me - half0), :]
+
+    def dispatch_x(m, owner):
+        @pl.loop(1, half)
+        def _(k):
+            x_copy(m, half_peer(k), owner).start()
+
+        rx[block(owner), :] = sx[m, block(me - half0), :]
+
+    sg[0] = (dot(pick, og[...], NN) * weight).astype(BF16)
+    dispatch_dy(0, me)
     local[1].wait()
-    mate_tok().start()
-    half_rows = pl.ds(pl.multiple_of(half0 * cp, cp), half * cp)
-    sx[0] = dot(pick_v[0, half_rows], tok[...], NN).astype(BF16)
-
-    @pl.loop(1, half)
-    def _(k):
-        x_copy(0, half_peer(k), me).start()
-
-    rx[block(me), :] = sx[0, block(me - half0), :]
+    mate_copy(1).start()
+    sx[0] = dot(pick, tok[...], NN).astype(BF16)
+    dispatch_x(0, me)
 
     grid = (gu.shape[3], lrows)
     line = lax.broadcasted_iota(jnp.int32, grid, 1)
@@ -286,17 +295,25 @@
         if j == own:
             rr[i, block(me), :] = rs[i, j, block(spot), :]
 
+    pick_v[0] = pick_of(ids, 0, rows)[0]
+    for i in range(1, n_dp):
+        ids_copy(i, dp_peer(i)).wait_recv()
+        pick_v[i] = pick_of(idsd.at[i - 1], 0, rows)[0]
+
+    mate_copy(2).wait_recv()
+    mate_copy(3).wait_recv()
+    pick2, weight2 = half_pick(ids2, probs2)
+    mate_copy(0).wait_recv()
+    sg[1] = (dot(pick2, og2[...], NN) * weight2).astype(BF16)
+    dispatch_dy(1, mate)
+
     local[2].wait()
     for i in range(1, n_dp):
         down_copy(i, dp_from(i), dp_peer(i)).wait_recv()
 
     for j in range(LEVELS):
 
-        @pl.loop(int(j == own), nl)
-        def _(t, j=j):
-            src = in_level(j, t)
-            dy_copy(src, src).wait_recv()
-
+        blocks(rg, nl - j % 2, dy_s.at[0], dy_r.at[j]).wait_recv()
         dyc[j] = dot(spr[...], rg[lpart(j), :], NN).astype(BF16)
         for f in range(0, hidden, fw):
             cols = slice(f, f + fw)
@@ -325,12 +342,9 @@
         proj_copy(i, dp_peer(i)).start()
     total[2] = term[rpart(my_dp), :]
 
-    for i in range(1, n_dp):
-        ids_copy(i, dp_peer(i)).wait_recv()
-        pick_v[i] = pick_of(idsd.at[i - 1], 0, rows)[0]
-    mate_ids().wait_recv()
-    pick2, _, _ = pick_of(ids2, half0, half * cp)
-    pick_m[...] = pick2
+    mate_copy(1).wait_recv()
+    sx[1] = dot(pick2, tok2[...], NN).astype(BF16)
+    dispatch_x(1, mate)
 
     def theirs(j):
         for i in range(1, n_dp):
@@ -339,25 +353,9 @@
 
     theirs(0)
 
-    mate_tok().wait_recv()
-    sx[1] = dot(pick_m[...], tok2[...], NN).astype(BF16)
-
-    @pl.loop(1, half)
-    def _(k):
-        x_copy(1, half_peer(k), mate).start()
-
-    rx[block(mate), :] = sx[1, block(me - half0), :]
-
     theirs(1)
 
-    @pl.loop(1, n_ex)
-    def _(k):
-        src = ex_peer(k)
-
-        @pl.when(src != mate)
-        def _():
-            x_copy(0, half0, src).wait_recv()
-
+    blocks(rx, n_ex - 2, x_s.at[0], x_r.at[0]).wait_recv()
     for j in range(LEVELS):
         xj = dot(spr[...], rx[lpart(j), :], NN).astype(BF16)
         if rk % 128:
@@ -372,7 +370,6 @@
         px_copy(i, dp_peer(i)).start()
 
     theirs(2)
-    theirs(3)
 
     def x_term(s, i):
         left = px.at[n_dp - 1 + i]
@@ -384,16 +381,14 @@
     stored = []
 
     def combine(i):
-        @pl.loop(1, n_ex)
-        def _(k):
-            src = ex_peer(k)
-            ret_copy(i, 0, src, src).wait_recv()
-
+        blocks(rr.at[i], n_ex - 1, ret_s.at[i], ret_r.at[i]).wait_recv()
         in_v[i] = dot(pick_v[i], rr[i], TN).astype(BF16)
 
     combine(0)
     stored.append(pltpu.make_async_copy(in_v.at[0], in_h.at[:, wpart(my_dp)], out_s.at[3]))
     stored[-1].start()
+
+    theirs(3)
     for i in range(1, n_dp):
         combine(i)
         in_copy(i, my_dp, dp_from(i)).start()
@@ -419,24 +414,13 @@
         proj_copy(i, dp_peer(i)).wait_send()
         for j in range(LEVELS):
             gu_copy(i, j, dp_peer(i)).wait_send()
-    mate_ids().wait_send()
-    mate_tok().wait_send()
-
-    @pl.loop(1, n_ex)
-    def _(k):
-        dy_copy(ex_peer(k), me).wait_send()
-
-    @pl.loop(1, half)
-    def _(k):
-        x_copy(0, half_peer(k), me).wait_send()
-        x_copy(1, half_peer(k), mate).wait_send()
-
+    for n in range(4):
+        mate_copy(n).wait_send()
+    for m in range(2):
+        blocks(rg, half - 1, dy_s.at[m], dy_r.at[0]).wait_send()
+        blocks(rx, half - 1, x_s.at[m], x_r.at[0]).wait_send()
     for i in range(n_dp):
-
-        @pl.loop(1, n_ex)
-        def _(k, i=i):
-            ret_copy(i, 0, ex_peer(k), me).wait_send()
-
+        blocks(rr.at[i], n_ex - 1, ret_s.at[i], ret_r.at[i]).wait_send()
     for copy in stored:
         copy.wait()
     for i in range(1, n_dp):
@@ -486,12 +470,13 @@
         pltpu.VMEM((tok_rows, width), BF16),
         pltpu.VMEM((tok_rows, width), BF16),
         pltpu.VMEM((tok_rows, width), BF16),
+        pltpu.VMEM((tok_rows, width), BF16),
         pltpu.VMEM((topk, tok_rows), jnp.int32),
+        pltpu.VMEM((topk, tok_rows), F32),
         pltpu.VMEM((n_dp - 1, topk, tok_rows), jnp.int32),
         pltpu.VMEM((n_dp, rows, tok_rows), BF16),
-        pltpu.VMEM((rows // 2, tok_rows), BF16),
         pltpu.VMEM((2, rows // 2, width), BF16),
-        pltpu.VMEM((rows, width), BF16),
+        pltpu.VMEM((2, rows // 2, width), BF16),
         pltpu.VMEM((rows, width), BF16),
         pltpu.VMEM((rows, width), BF16),
         pltpu.VMEM((LEVELS, lpad, width), BF16),
@@ -515,9 +500,9 @@
         pltpu.VMEM((rank, hidden), F32),
         pltpu.VMEM((3, rk, hidden), F32),
         dma((8,)), dma((LEVELS,)),
-        dma((n_ex,)), dma((n_ex,)), dma((2, n_ex // 2)), dma((n_ex,)), dma, dma,
+        dma((2,)), dma((LEVELS,)), dma((2,)), dma((1,)), dma((4,)), dma((4,)),
         dma((n_dp,)), dma((n_dp,)), dma((n_dp,)), dma((n_dp,)),
-        dma((n_dp, LEVELS)), dma((n_dp, LEVELS)), dma((n_dp, n_ex)), dma((n_dp, n_ex)),
+        dma((n_dp, LEVELS)), dma((n_dp, LEVELS)), dma((n_dp,)), dma((n_dp,)),
         dma((n_dp,)), dma((n_dp,)), dma((n_dp,)), dma((n_dp,)),
         dma((n_dp,)), dma((n_dp,)), dma((n_dp,)), dma((n_dp,)), dma((4,)),
     ]

time: 79.3 us -> 79.4 us (level)
  no operation moved by 1% of the time
where the time goes in v3:
time: 79.4 us; the launch traced here: 79.2 us
  Pallas kernels  78.6 us (99%)
    pallas_call x1, Pallas kernels, body(): pl.pallas_call(functools.partial(kernel, n_dp, n_ex, cap, cp), out_shape=...  76.4 us
    pallas_call x1, Pallas kernels, body(): pl.pallas_call(finish, out_shape=(jax.ShapeDtypeStruct((tok_rows, width),...  2.16 us

profile of v3, /device:TPU:0, one launch (start us, length us, event | category | flops | bytes accessed | tf_op | source)
XLA Modules:
  0.0 79.2 jit_solution(2295927121435225255)
XLA Ops:
  0.6 76.4 %shard_map.104 = (bf16[128,1024]{1,0:T(8,128)(2,1)}, f32[3,128,768]{2,1,0:T(8,128)}) custom-call(s32[3,128]{1,0:T(4,128)} %bitcast.2, f32[3,128]{1,0:T(4,128)} %bitcast.3, bf16[128,1024]{1,0:T(8,128)(2,1)} %tok_h.1, bf16[128,1024]{1,0:T(8,128)(2,1)} %og_h.1, bf16[1,1,480,1536]{3,2,1,0:T(8,128)(2,1)} %pre_h.1, bf16[1,512,768]{2,1,0:T(8,128)(2,1)} %gw_h.1, ...), custom_call_target="tpu_custom_call" | custom-call | tf_op jit(solution)/shard_map/pallas_call | solution.py:509
  77.1 2.2 %shard_map.105 = (bf16[128,1024]{1,0:T(8,128)(2,1)}, f32[1,3,128,768]{3,2,1,0:T(8,128)}) custom-call(bf16[128,1024]{1,0:T(8,128)(2,1)} %get-tuple-element.4.in_h, f32[3,128,768]{2,1,0:T(8,128)} %get-tuple-element.5.proj_h), custom_call_target="tpu_custom_call" | custom-call | tf_op jit(solution)/shard_map/pallas_call | solution.py:525

commit v4 on v3

--- a/solution.py
+++ b/solution.py
@@ -232,6 +232,8 @@
         )
 
     for i in range(1, n_dp):
+        ids_copy(i, dp_peer(i)).start()
+    for i in range(1, n_dp):
         down_copy(i, my_dp, dp_peer(i)).start()
     mate_copy(2).start()
     mate_copy(3).start()
@@ -239,8 +241,6 @@
     mate_copy(0).start()
     for i in range(1, n_dp):
         base_copy(i, my_dp, dp_peer(i)).start()
-    for i in range(1, n_dp):
-        ids_copy(i, dp_peer(i)).start()
 
     def dispatch_dy(m, owner):
         for near, tag in ((0, 0 if m == 0 else 2), (own, own if m == 0 else 1)):

time: 79.4 us -> 76.5 us (0.963)
  Pallas kernels: 78.6 us -> 75.7 us
    pallas_call x1, Pallas kernels: 76.4 us -> 73.5 us  [body(): pl.pallas_call(functools.partial(kernel, n_dp, n_ex, cap, cp), out_shape=...]
where the time goes in v4:
time: 76.5 us; the launch traced here: 76.3 us
  Pallas kernels  75.7 us (99%)
    pallas_call x1, Pallas kernels, body(): pl.pallas_call(functools.partial(kernel, n_dp, n_ex, cap, cp), out_shape=...  73.5 us
    pallas_call x1, Pallas kernels, body(): pl.pallas_call(finish, out_shape=(jax.ShapeDtypeStruct((tok_rows, width),...  2.16 us

profile of v4, /device:TPU:0, one launch (start us, length us, event | category | flops | bytes accessed | tf_op | source)
XLA Modules:
  0.0 76.3 jit_solution(16301077796193902663)
XLA Ops:
  0.6 73.5 %shard_map.104 = (bf16[128,1024]{1,0:T(8,128)(2,1)}, f32[3,128,768]{2,1,0:T(8,128)}) custom-call(s32[3,128]{1,0:T(4,128)} %bitcast.2, f32[3,128]{1,0:T(4,128)} %bitcast.3, bf16[128,1024]{1,0:T(8,128)(2,1)} %tok_h.1, bf16[128,1024]{1,0:T(8,128)(2,1)} %og_h.1, bf16[1,1,480,1536]{3,2,1,0:T(8,128)(2,1)} %pre_h.1, bf16[1,512,768]{2,1,0:T(8,128)(2,1)} %gw_h.1, ...), custom_call_target="tpu_custom_call" | custom-call | tf_op jit(solution)/shard_map/pallas_call | solution.py:509
  74.1 2.2 %shard_map.105 = (bf16[128,1024]{1,0:T(8,128)(2,1)}, f32[1,3,128,768]{3,2,1,0:T(8,128)}) custom-call(bf16[128,1024]{1,0:T(8,128)(2,1)} %get-tuple-element.4.in_h, f32[3,128,768]{2,1,0:T(8,128)} %get-tuple-element.5.proj_h), custom_call_target="tpu_custom_call" | custom-call | tf_op jit(solution)/shard_map/pallas_call | solution.py:525

commit v5 on v4

--- a/solution.py
+++ b/solution.py
@@ -10,6 +10,7 @@
 F32 = jnp.float32
 BF16 = jnp.bfloat16
 LEVELS = 4
+VMEM_BYTES = 67043328
 
 
 def dot(left, right, dims):
@@ -24,11 +25,11 @@
 def kernel(
     n_dp, n_ex, cap, cp,
     ids_h, probs_h, tok_h, og_h, pre_h, gw_h, uw_h, dw, bs,
-    in_h, proj_h,
+    in_out, total,
     ids, probs, tok, og, tok2, og2, ids2, probs2, idsd, pick_v, sx, sg, rx, rg, dyc, spr, dfull, bfull, gw, uw, pre,
-    act_a, act_b, hid, gu, px, pdy, rs, rr, in_v, psend, prec, term, total,
+    act_a, act_b, hid, gu, px, pdy, rs, rr, in_v, psend, prec, term,
     local_sem, pre_sem, dy_s, dy_r, x_s, x_r, mate_s, mate_r, down_s, down_r, base_s, base_r,
-    gu_s, gu_r, ret_s, ret_r, px_s, px_r, proj_s, proj_r, in_s, in_r, ids_s, ids_r, out_s,
+    gu_s, gu_r, ret_s, ret_r, px_s, px_r, proj_s, proj_r, in_s, in_r, ids_s, ids_r,
 ):
     my_dp = lax.axis_index("dp")
     me = lax.axis_index("expert")
@@ -227,7 +228,7 @@
 
     def in_copy(i, owner, peer):
         return pltpu.make_async_remote_copy(
-            in_v.at[i], in_h.at[:, wpart(owner)], in_s.at[i], in_r.at[i],
+            in_v.at[i - 1], in_out.at[:, wpart(owner)], in_s.at[i], in_r.at[i],
             device_id={"dp": peer}, device_id_type=MESH,
         )
 
@@ -378,33 +379,24 @@
     for s in range(2):
         total[s] = x_term(s, 0)
 
-    stored = []
-
     def combine(i):
         blocks(rr.at[i], n_ex - 1, ret_s.at[i], ret_r.at[i]).wait_recv()
-        in_v[i] = dot(pick_v[i], rr[i], TN).astype(BF16)
-
-    combine(0)
-    stored.append(pltpu.make_async_copy(in_v.at[0], in_h.at[:, wpart(my_dp)], out_s.at[3]))
-    stored[-1].start()
+        return dot(pick_v[i], rr[i], TN).astype(BF16)
+
+    in_out[:, wpart(my_dp)] = combine(0)
 
     theirs(3)
     for i in range(1, n_dp):
-        combine(i)
+        in_v[i - 1] = combine(i)
         in_copy(i, my_dp, dp_from(i)).start()
 
     for i in range(1, n_dp):
         proj_copy(i, dp_peer(i)).wait_recv()
         total[2] += prec[i - 1].astype(F32)
-    stored.append(pltpu.make_async_copy(total.at[2], proj_h.at[2], out_s.at[2]))
-    stored[-1].start()
     for i in range(1, n_dp):
         px_copy(i, dp_peer(i)).wait_recv()
         for s in range(2):
             total[s] += x_term(s, i)
-    for s in range(2):
-        stored.append(pltpu.make_async_copy(total.at[s], proj_h.at[s], out_s.at[s]))
-        stored[-1].start()
 
     for i in range(1, n_dp):
         down_copy(i, my_dp, dp_peer(i)).wait_send()
@@ -421,27 +413,18 @@
         blocks(rx, half - 1, x_s.at[m], x_r.at[0]).wait_send()
     for i in range(n_dp):
         blocks(rr.at[i], n_ex - 1, ret_s.at[i], ret_r.at[i]).wait_send()
-    for copy in stored:
-        copy.wait()
     for i in range(1, n_dp):
         in_copy(i, my_dp, dp_from(i)).wait_send()
         in_copy(i, dp_peer(i), dp_from(i)).wait_recv()
 
 
-def finish(in_h, proj_h, in_ref, proj_ref, rows, proj, load_s, store_s):
-    n = proj.shape[0]
-    loads = [pltpu.make_async_copy(proj_h.at[t], proj.at[t], load_s.at[t]) for t in range(n)]
-    loads.append(pltpu.make_async_copy(in_h, rows, load_s.at[n]))
-    stores = [
-        pltpu.make_async_copy(proj.at[t], proj_ref.at[0, t], store_s.at[t]) for t in range(n)
-    ]
-    stores.append(pltpu.make_async_copy(rows, in_ref, store_s.at[n]))
-    for copy in loads:
+def finish(in_h, proj_h, in_ref, proj_ref, sems):
+    n = proj_h.shape[0]
+    copies = [pltpu.make_async_copy(proj_h.at[t], proj_ref.at[0, t], sems.at[t]) for t in range(n)]
+    copies.append(pltpu.make_async_copy(in_h, in_ref, sems.at[n]))
+    for copy in copies:
         copy.start()
-    for load, store in zip(loads, stores):
-        load.wait()
-        store.start()
-    for copy in stores:
+    for copy in copies:
         copy.wait()
 
 
@@ -462,6 +445,7 @@
     part = gate_weight.shape[1]
     rank = basis.shape[2]
     rk = rank // n_dp
+    vmem = pl.BlockSpec(memory_space=pltpu.VMEM)
     hbm = pl.BlockSpec(memory_space=pl.ANY)
     dma = pltpu.SemaphoreType.DMA
     scratch = [
@@ -494,29 +478,26 @@
         pltpu.VMEM((LEVELS, lpad, rank), BF16),
         pltpu.VMEM((n_dp, LEVELS, lrows, part), BF16),
         pltpu.VMEM((n_dp, rows, part), BF16),
-        pltpu.VMEM((n_dp, tok_rows, part), BF16),
+        pltpu.VMEM((n_dp - 1, tok_rows, part), BF16),
         pltpu.VMEM((n_dp - 1, rk, hidden), BF16),
         pltpu.VMEM((n_dp - 1, rk, hidden), BF16),
         pltpu.VMEM((rank, hidden), F32),
-        pltpu.VMEM((3, rk, hidden), F32),
         dma((8,)), dma((LEVELS,)),
         dma((2,)), dma((LEVELS,)), dma((2,)), dma((1,)), dma((4,)), dma((4,)),
         dma((n_dp,)), dma((n_dp,)), dma((n_dp,)), dma((n_dp,)),
         dma((n_dp, LEVELS)), dma((n_dp, LEVELS)), dma((n_dp,)), dma((n_dp,)),
         dma((n_dp,)), dma((n_dp,)), dma((n_dp,)), dma((n_dp,)),
-        dma((n_dp,)), dma((n_dp,)), dma((n_dp,)), dma((n_dp,)), dma((4,)),
+        dma((n_dp,)), dma((n_dp,)), dma((n_dp,)), dma((n_dp,)),
     ]
+    outputs = tok_rows * width * 2 + 3 * rk * hidden * 4
     in_part, proj = pl.pallas_call(
         functools.partial(kernel, n_dp, n_ex, cap, cp),
-        out_shape=(
-            jax.ShapeDtypeStruct((tok_rows, width), BF16),
-            jax.ShapeDtypeStruct((3, rk, hidden), F32),
-        ),
+        out_shape=(pltpu.VMEM((tok_rows, width), BF16), pltpu.VMEM((3, rk, hidden), F32)),
         in_specs=[hbm] * 9,
-        out_specs=(hbm, hbm),
+        out_specs=(vmem, vmem),
         scratch_shapes=scratch,
         compiler_params=pltpu.CompilerParams(
-            collective_id=0, has_side_effects=True, vmem_limit_bytes=60 * 1024 * 1024
+            collective_id=0, has_side_effects=True, vmem_limit_bytes=VMEM_BYTES - outputs
         ),
     )(
         expert_ids.T, gate_probs.T, tokens, out_grad, saved_pre,
@@ -530,11 +511,8 @@
         ),
         in_specs=[hbm, hbm],
         out_specs=(hbm, hbm),
-        scratch_shapes=[
-            pltpu.VMEM((tok_rows, width), BF16),
-            pltpu.VMEM((3, rk, hidden), F32),
-            dma((4,)), dma((4,)),
-        ],
+        scratch_shapes=[dma((4,))],
+        compiler_params=pltpu.CompilerParams(vmem_limit_bytes=1024 * 1024),
     )(in_part, proj)
 
 

time: 76.5 us -> 75.3 us (0.984)
  Pallas kernels: 75.7 us -> 74.5 us
    pallas_call x1, Pallas kernels: 2.16 us -> 1.13 us  [body(): pl.pallas_call(finish, out_shape=(jax.ShapeDtypeStruct((tok_rows, width),...]
where the time goes in v5:
time: 75.3 us; the launch traced here: 75.1 us
  Pallas kernels  74.5 us (99%)
    pallas_call x1, Pallas kernels, body(): pl.pallas_call(functools.partial(kernel, n_dp, n_ex, cap, cp), out_shape=...  73.4 us

profile of v5, /device:TPU:0, one launch (start us, length us, event | category | flops | bytes accessed | tf_op | source)
XLA Modules:
  0.0 75.1 jit_solution(6645238005137898982)
XLA Ops:
  0.6 73.4 %shard_map.104 = (bf16[128,1024]{1,0:T(8,128)(2,1)S(1)}, f32[3,128,768]{2,1,0:T(8,128)S(1)}) custom-call(s32[3,128]{1,0:T(4,128)} %bitcast.2, f32[3,128]{1,0:T(4,128)} %bitcast.3, bf16[128,1024]{1,0:T(8,128)(2,1)} %tok_h.1, bf16[128,1024]{1,0:T(8,128)(2,1)} %og_h.1, bf16[1,1,480,1536]{3,2,1,0:T(8,128)(2,1)} %pre_h.1, bf16[1,512,768]{2,1,0:T(8,128)(2,1)} %gw_h.1, ...), custom_call_target="tpu_custom_call" | custom-call | tf_op jit(solution)/shard_map/pallas_call | solution.py:493
  74.0 1.1 %shard_map.105 = (bf16[128,1024]{1,0:T(8,128)(2,1)}, f32[1,3,128,768]{3,2,1,0:T(8,128)}) custom-call(bf16[128,1024]{1,0:T(8,128)(2,1)S(1)} %get-tuple-element.4.in_h, f32[3,128,768]{2,1,0:T(8,128)S(1)} %get-tuple-element.5.proj_h), custom_call_target="tpu_custom_call" | custom-call | tf_op jit(solution)/shard_map/pallas_call | solution.py:506

commit v6 on v5

--- a/solution.py
+++ b/solution.py
@@ -29,7 +29,7 @@
     ids, probs, tok, og, tok2, og2, ids2, probs2, idsd, pick_v, sx, sg, rx, rg, dyc, spr, dfull, bfull, gw, uw, pre,
     act_a, act_b, hid, gu, px, pdy, rs, rr, in_v, psend, prec, term,
     local_sem, pre_sem, dy_s, dy_r, x_s, x_r, mate_s, mate_r, down_s, down_r, base_s, base_r,
-    gu_s, gu_r, ret_s, ret_r, px_s, px_r, proj_s, proj_r, in_s, in_r, ids_s, ids_r,
+    gu_s, gu_r, ret_s, ret_r, px_s, px_r, proj_s, proj_r, in_s, in_r, ids_s, ids_r, ready,
 ):
     my_dp = lax.axis_index("dp")
     me = lax.axis_index("expert")
@@ -106,9 +106,16 @@
     for i in range(1, n_dp):
         pl.semaphore_signal(barrier, inc=1, device_id={"dp": dp_peer(i)}, device_id_type=MESH)
 
-    @pl.loop(1, n_ex)
+    odd = lax.rem(me, 2)
+
+    @pl.loop(odd, half)
     def _(k):
-        pl.semaphore_signal(barrier, inc=1, device_id={"expert": ex_peer(k)}, device_id_type=MESH)
+        hub = lax.rem(me + 1 - odd + 2 * k, n_ex)
+        pl.semaphore_signal(barrier, inc=1, device_id={"expert": hub}, device_id_type=MESH)
+
+    @pl.when(odd == 1)
+    def _():
+        pl.semaphore_signal(barrier, inc=1, device_id={"expert": me - 1}, device_id_type=MESH)
 
     local = [
         pltpu.make_async_copy(og_h, og, local_sem.at[0]),
@@ -156,7 +163,7 @@
         copy.wait()
     pick, weight = half_pick(ids, probs)
 
-    pl.semaphore_wait(barrier, n_ex - 1 + n_dp - 1)
+    pl.semaphore_wait(barrier, n_dp + odd * (n_ex - 2))
 
     def down_copy(i, owner, peer):
         return pltpu.make_async_remote_copy(
@@ -236,12 +243,23 @@
         ids_copy(i, dp_peer(i)).start()
     for i in range(1, n_dp):
         down_copy(i, my_dp, dp_peer(i)).start()
+    for i in range(1, n_dp):
+        base_copy(i, my_dp, dp_peer(i)).start()
+
+    @pl.when(odd == 1)
+    def _():
+        pl.semaphore_signal(ready, inc=1, device_id={"expert": me - 1}, device_id_type=MESH)
+
+    local[0].wait()
+    sg[0] = (dot(pick, og[...], NN) * weight).astype(BF16)
+
+    @pl.when(odd == 0)
+    def _():
+        pl.semaphore_wait(ready, 1)
+
     mate_copy(2).start()
     mate_copy(3).start()
-    local[0].wait()
     mate_copy(0).start()
-    for i in range(1, n_dp):
-        base_copy(i, my_dp, dp_peer(i)).start()
 
     def dispatch_dy(m, owner):
         for near, tag in ((0, 0 if m == 0 else 2), (own, own if m == 0 else 1)):
@@ -259,7 +277,6 @@
 
         rx[block(owner), :] = sx[m, block(me - half0), :]
 
-    sg[0] = (dot(pick, og[...], NN) * weight).astype(BF16)
     dispatch_dy(0, me)
     local[1].wait()
     mate_copy(1).start()
@@ -488,6 +505,7 @@
         dma((n_dp, LEVELS)), dma((n_dp, LEVELS)), dma((n_dp,)), dma((n_dp,)),
         dma((n_dp,)), dma((n_dp,)), dma((n_dp,)), dma((n_dp,)),
         dma((n_dp,)), dma((n_dp,)), dma((n_dp,)), dma((n_dp,)),
+        pltpu.SemaphoreType.REGULAR,
     ]
     outputs = tok_rows * width * 2 + 3 * rk * hidden * 4
     in_part, proj = pl.pallas_call(

time: 75.3 us -> 72.8 us (0.967)
  Pallas kernels: 74.5 us -> 72 us
    pallas_call x1, Pallas kernels: 73.4 us -> 70.8 us  [body(): pl.pallas_call(functools.partial(kernel, n_dp, n_ex, cap, cp), out_shape=...]
where the time goes in v6:
time: 72.8 us; the launch traced here: 72.6 us
  Pallas kernels  72 us (99%)
    pallas_call x1, Pallas kernels, body(): pl.pallas_call(functools.partial(kernel, n_dp, n_ex, cap, cp), out_shape=...  70.8 us

profile of v6, /device:TPU:0, one launch (start us, length us, event | category | flops | bytes accessed | tf_op | source)
XLA Modules:
  0.0 72.6 jit_solution(4797386242193447279)
XLA Ops:
  0.6 70.8 %shard_map.104 = (bf16[128,1024]{1,0:T(8,128)(2,1)S(1)}, f32[3,128,768]{2,1,0:T(8,128)S(1)}) custom-call(s32[3,128]{1,0:T(4,128)} %bitcast.2, f32[3,128]{1,0:T(4,128)} %bitcast.3, bf16[128,1024]{1,0:T(8,128)(2,1)} %tok_h.1, bf16[128,1024]{1,0:T(8,128)(2,1)} %og_h.1, bf16[1,1,480,1536]{3,2,1,0:T(8,128)(2,1)} %pre_h.1, bf16[1,512,768]{2,1,0:T(8,128)(2,1)} %gw_h.1, ...), custom_call_target="tpu_custom_call" | custom-call | tf_op jit(solution)/shard_map/pallas_call | solution.py:511
  71.5 1.1 %shard_map.105 = (bf16[128,1024]{1,0:T(8,128)(2,1)}, f32[1,3,128,768]{3,2,1,0:T(8,128)}) custom-call(bf16[128,1024]{1,0:T(8,128)(2,1)S(1)} %get-tuple-element.4.in_h, f32[3,128,768]{2,1,0:T(8,128)S(1)} %get-tuple-element.5.proj_h), custom_call_target="tpu_custom_call" | custom-call | tf_op jit(solution)/shard_map/pallas_call | solution.py:524

commit v7 on v6

--- a/solution.py
+++ b/solution.py
@@ -98,6 +98,7 @@
         for j in range(LEVELS):
             pre[j, lcap:, :] = jnp.zeros((pad, 2 * hidden), BF16)
             for i in range(1, n_dp):
+                px[n_dp - 1 + i, j, lcap:, :] = jnp.zeros((pad, rk), BF16)
                 for s in range(2):
                     gu[i, j, s, lcap:, :] = jnp.zeros((pad, hidden), BF16)
 
@@ -134,6 +135,94 @@
     for copy in local[:2] + pre_copy + local[2:]:
         copy.start()
 
+    def down_copy(i, owner, peer):
+        return pltpu.make_async_remote_copy(
+            dw.at[0], dfull.at[wpart(owner)], down_s.at[i], down_r.at[i],
+            device_id={"dp": peer}, device_id_type=MESH,
+        )
+
+    def base_copy(i, owner, peer):
+        return pltpu.make_async_remote_copy(
+            bs.at[0], bfull.at[wpart(owner)], base_s.at[i], base_r.at[i],
+            device_id={"dp": peer}, device_id_type=MESH,
+        )
+
+    def ids_copy(i, peer):
+        return pltpu.make_async_remote_copy(
+            ids_h, idsd.at[i - 1], ids_s.at[i], ids_r.at[i],
+            device_id={"dp": peer}, device_id_type=MESH,
+        )
+
+    def mate_copy(n):
+        src, dst = ((og, og2), (tok, tok2), (ids, ids2), (probs, probs2))[n]
+        return pltpu.make_async_remote_copy(
+            src, dst, mate_s.at[n], mate_r.at[n], device_id={"expert": mate}, device_id_type=MESH
+        )
+
+    def dy_copy(m, peer, owner, j):
+        return pltpu.make_async_remote_copy(
+            sg.at[m, block(peer - half0)], rg.at[block(owner)], dy_s.at[m], dy_r.at[j],
+            device_id={"expert": peer}, device_id_type=MESH,
+        )
+
+    def x_copy(m, peer, owner):
+        return pltpu.make_async_remote_copy(
+            sx.at[m, block(peer - half0)], rx.at[block(owner)], x_s.at[m], x_r.at[0],
+            device_id={"expert": peer}, device_id_type=MESH,
+        )
+
+    def blocks(buffer, count, send, recv):
+        span = buffer.at[pl.ds(0, count * cp)]
+        return pltpu.make_async_remote_copy(
+            span, span, send, recv, device_id={"expert": mate}, device_id_type=MESH
+        )
+
+    used = pl.ds(0, lcap)
+
+    def gu_copy(i, j, peer):
+        return pltpu.make_async_remote_copy(
+            gu.at[0, j, :, used], gu.at[i, j, :, used], gu_s.at[i, j], gu_r.at[i, j],
+            device_id={"dp": peer}, device_id_type=MESH,
+        )
+
+    def px_copy(i, peer):
+        return pltpu.make_async_remote_copy(
+            px.at[i - 1, :, used], px.at[n_dp - 1 + i, :, used], px_s.at[i], px_r.at[i],
+            device_id={"dp": peer}, device_id_type=MESH,
+        )
+
+    def ret_copy(i, j, peer, owner):
+        return pltpu.make_async_remote_copy(
+            rs.at[i, j, block(lax.rem(peer, nl))], rr.at[i, block(owner)],
+            ret_s.at[i], ret_r.at[i],
+            device_id={"expert": peer}, device_id_type=MESH,
+        )
+
+    def proj_copy(i, peer):
+        return pltpu.make_async_remote_copy(
+            psend.at[i - 1], prec.at[i - 1], proj_s.at[i], proj_r.at[i],
+            device_id={"dp": peer}, device_id_type=MESH,
+        )
+
+    def in_copy(i, owner, peer):
+        return pltpu.make_async_remote_copy(
+            in_v.at[i - 1], in_out.at[owner], in_s.at[i], in_r.at[i],
+            device_id={"dp": peer}, device_id_type=MESH,
+        )
+
+    def start_dp():
+        for i in range(1, n_dp):
+            ids_copy(i, dp_peer(i)).start()
+        for i in range(1, n_dp):
+            down_copy(i, my_dp, dp_peer(i)).start()
+        for i in range(1, n_dp):
+            base_copy(i, my_dp, dp_peer(i)).start()
+
+    @pl.when(odd == 0)
+    def _():
+        pl.semaphore_wait(barrier, n_dp)
+        start_dp()
+
     one, zero = jnp.ones((), F32), jnp.zeros((), F32)
     earlier = lax.broadcasted_iota(jnp.int32, (tokens, tokens), 0) < lax.broadcasted_iota(
         jnp.int32, (tokens, tokens), 1
@@ -163,95 +252,14 @@
         copy.wait()
     pick, weight = half_pick(ids, probs)
 
-    pl.semaphore_wait(barrier, n_dp + odd * (n_ex - 2))
-
-    def down_copy(i, owner, peer):
-        return pltpu.make_async_remote_copy(
-            dw.at[0], dfull.at[wpart(owner)], down_s.at[i], down_r.at[i],
-            device_id={"dp": peer}, device_id_type=MESH,
-        )
-
-    def base_copy(i, owner, peer):
-        return pltpu.make_async_remote_copy(
-            bs.at[0], bfull.at[wpart(owner)], base_s.at[i], base_r.at[i],
-            device_id={"dp": peer}, device_id_type=MESH,
-        )
-
-    def ids_copy(i, peer):
-        return pltpu.make_async_remote_copy(
-            ids, idsd.at[i - 1], ids_s.at[i], ids_r.at[i],
-            device_id={"dp": peer}, device_id_type=MESH,
-        )
-
-    def mate_copy(n):
-        src, dst = ((og, og2), (tok, tok2), (ids, ids2), (probs, probs2))[n]
-        return pltpu.make_async_remote_copy(
-            src, dst, mate_s.at[n], mate_r.at[n], device_id={"expert": mate}, device_id_type=MESH
-        )
-
-    def dy_copy(m, peer, owner, j):
-        return pltpu.make_async_remote_copy(
-            sg.at[m, block(peer - half0)], rg.at[block(owner)], dy_s.at[m], dy_r.at[j],
-            device_id={"expert": peer}, device_id_type=MESH,
-        )
-
-    def x_copy(m, peer, owner):
-        return pltpu.make_async_remote_copy(
-            sx.at[m, block(peer - half0)], rx.at[block(owner)], x_s.at[m], x_r.at[0],
-            device_id={"expert": peer}, device_id_type=MESH,
-        )
-
-    def blocks(buffer, count, send, recv):
-        span = buffer.at[pl.ds(0, count * cp)]
-        return pltpu.make_async_remote_copy(
-            span, span, send, recv, device_id={"expert": mate}, device_id_type=MESH
-        )
-
-    def gu_copy(i, j, peer):
-        used = pl.ds(0, lcap)
-        return pltpu.make_async_remote_copy(
-            gu.at[0, j, :, used], gu.at[i, j, :, used], gu_s.at[i, j], gu_r.at[i, j],
-            device_id={"dp": peer}, device_id_type=MESH,
-        )
-
-    def px_copy(i, peer):
-        return pltpu.make_async_remote_copy(
-            px.at[i - 1], px.at[n_dp - 1 + i], px_s.at[i], px_r.at[i],
-            device_id={"dp": peer}, device_id_type=MESH,
-        )
-
-    def ret_copy(i, j, peer, owner):
-        return pltpu.make_async_remote_copy(
-            rs.at[i, j, block(lax.rem(peer, nl))], rr.at[i, block(owner)],
-            ret_s.at[i], ret_r.at[i],
-            device_id={"expert": peer}, device_id_type=MESH,
-        )
-
-    def proj_copy(i, peer):
-        return pltpu.make_async_remote_copy(
-            psend.at[i - 1], prec.at[i - 1], proj_s.at[i], proj_r.at[i],
-            device_id={"dp": peer}, device_id_type=MESH,
-        )
-
-    def in_copy(i, owner, peer):
-        return pltpu.make_async_remote_copy(
-            in_v.at[i - 1], in_out.at[:, wpart(owner)], in_s.at[i], in_r.at[i],
-            device_id={"dp": peer}, device_id_type=MESH,
-        )
-
-    for i in range(1, n_dp):
-        ids_copy(i, dp_peer(i)).start()
-    for i in range(1, n_dp):
-        down_copy(i, my_dp, dp_peer(i)).start()
-    for i in range(1, n_dp):
-        base_copy(i, my_dp, dp_peer(i)).start()
+    local[0].wait()
+    sg[0] = (dot(pick, og[...], NN) * weight).astype(BF16)
 
     @pl.when(odd == 1)
     def _():
+        pl.semaphore_wait(barrier, n_dp + n_ex - 2)
+        start_dp()
         pl.semaphore_signal(ready, inc=1, device_id={"expert": me - 1}, device_id_type=MESH)
-
-    local[0].wait()
-    sg[0] = (dot(pick, og[...], NN) * weight).astype(BF16)
 
     @pl.when(odd == 0)
     def _():
@@ -278,11 +286,6 @@
         rx[block(owner), :] = sx[m, block(me - half0), :]
 
     dispatch_dy(0, me)
-    local[1].wait()
-    mate_copy(1).start()
-    sx[0] = dot(pick, tok[...], NN).astype(BF16)
-    dispatch_x(0, me)
-
     grid = (gu.shape[3], lrows)
     line = lax.broadcasted_iota(jnp.int32, grid, 1)
     inner = lax.bitwise_and(line, cp - 1)
@@ -324,6 +327,11 @@
     mate_copy(0).wait_recv()
     sg[1] = (dot(pick2, og2[...], NN) * weight2).astype(BF16)
     dispatch_dy(1, mate)
+
+    local[1].wait()
+    mate_copy(1).start()
+    sx[0] = dot(pick, tok[...], NN).astype(BF16)
+    dispatch_x(0, me)
 
     local[2].wait()
     for i in range(1, n_dp):
@@ -357,7 +365,6 @@
     term[...] = project(lambda j: pdy[j], lambda j: hid[j])
     for i in range(1, n_dp):
         psend[i - 1] = term[rpart(dp_peer(i)), :].astype(BF16)
-        proj_copy(i, dp_peer(i)).start()
     total[2] = term[rpart(my_dp), :]
 
     mate_copy(1).wait_recv()
@@ -367,6 +374,8 @@
     def theirs(j):
         for i in range(1, n_dp):
             gu_copy(i, j, dp_peer(i)).wait_recv()
+            if j == own and i == n_dp - 1:
+                pl.when(odd == 0)(start_projections)
             row_grad(i, j)
 
     theirs(0)
@@ -384,8 +393,13 @@
             else:
                 pj = dot(xj, bfull[:, rpart(dp_peer(i))], NN)
             px[(i + n_dp - 1) % n_dp, j] = pj.astype(BF16)
-    for i in range(1, n_dp):
-        px_copy(i, dp_peer(i)).start()
+
+    def start_projections():
+        for i in range(1, n_dp):
+            proj_copy(i, dp_peer(i)).start()
+            px_copy(i, dp_peer(i)).start()
+
+    pl.when(odd == 1)(start_projections)
 
     theirs(2)
 
@@ -400,7 +414,7 @@
         blocks(rr.at[i], n_ex - 1, ret_s.at[i], ret_r.at[i]).wait_recv()
         return dot(pick_v[i], rr[i], TN).astype(BF16)
 
-    in_out[:, wpart(my_dp)] = combine(0)
+    in_out[my_dp] = combine(0)
 
     theirs(3)
     for i in range(1, n_dp):
@@ -435,10 +449,13 @@
         in_copy(i, dp_peer(i), dp_from(i)).wait_recv()
 
 
-def finish(in_h, proj_h, in_ref, proj_ref, sems):
+def finish(in_h, proj_h, in_ref, proj_ref, proj_s, in_s):
+    parts, _, part = in_h.shape
     n = proj_h.shape[0]
-    copies = [pltpu.make_async_copy(proj_h.at[t], proj_ref.at[0, t], sems.at[t]) for t in range(n)]
-    copies.append(pltpu.make_async_copy(in_h, in_ref, sems.at[n]))
+    copies = [pltpu.make_async_copy(proj_h.at[t], proj_ref.at[0, t], proj_s.at[t]) for t in range(n)]
+    for d in range(parts):
+        cols = pl.ds(d * part, part)
+        copies.append(pltpu.make_async_copy(in_h.at[d], in_ref.at[:, cols], in_s.at[d]))
     for copy in copies:
         copy.start()
     for copy in copies:
@@ -510,7 +527,7 @@
     outputs = tok_rows * width * 2 + 3 * rk * hidden * 4
     in_part, proj = pl.pallas_call(
         functools.partial(kernel, n_dp, n_ex, cap, cp),
-        out_shape=(pltpu.VMEM((tok_rows, width), BF16), pltpu.VMEM((3, rk, hidden), F32)),
+        out_shape=(pltpu.VMEM((n_dp, tok_rows, part), BF16), pltpu.VMEM((3, rk, hidden), F32)),
         in_specs=[hbm] * 9,
         out_specs=(vmem, vmem),
         scratch_shapes=scratch,
@@ -529,7 +546,7 @@
         ),
         in_specs=[hbm, hbm],
         out_specs=(hbm, hbm),
-        scratch_shapes=[dma((4,))],
+        scratch_shapes=[dma((3,)), dma((n_dp,))],
         compiler_params=pltpu.CompilerParams(vmem_limit_bytes=1024 * 1024),
     )(in_part, proj)
 

time: 72.8 us -> 72 us (0.989)
  Pallas kernels: 72 us -> 71.2 us
    pallas_call x1, Pallas kernels: 70.8 us -> 70.1 us  [body(): pl.pallas_call(functools.partial(kernel, n_dp, n_ex, cap, cp), out_shape=...]
where the time goes in v7:
time: 72 us; the launch traced here: 71.9 us
  Pallas kernels  71.2 us (99%)
    pallas_call x1, Pallas kernels, body(): pl.pallas_call(functools.partial(kernel, n_dp, n_ex, cap, cp), out_shape=...  70.1 us

profile of v7, /device:TPU:0, one launch (start us, length us, event | category | flops | bytes accessed | tf_op | source)
XLA Modules:
  0.0 71.9 jit_solution(12830666751025837830)
XLA Ops:
  0.6 70.1 %shard_map.104 = (bf16[2,128,512]{2,1,0:T(8,128)(2,1)S(1)}, f32[3,128,768]{2,1,0:T(8,128)S(1)}) custom-call(s32[3,128]{1,0:T(4,128)} %bitcast.2, f32[3,128]{1,0:T(4,128)} %bitcast.3, bf16[128,1024]{1,0:T(8,128)(2,1)} %tok_h.1, bf16[128,1024]{1,0:T(8,128)(2,1)} %og_h.1, bf16[1,1,480,1536]{3,2,1,0:T(8,128)(2,1)} %pre_h.1, bf16[1,512,768]{2,1,0:T(8,128)(2,1)} %gw_h.1, ...), custom_call_target="tpu_custom_call" | custom-call | tf_op jit(solution)/shard_map/pallas_call | solution.py:528
  70.8 1.1 %shard_map.105 = (bf16[128,1024]{1,0:T(8,128)(2,1)}, f32[1,3,128,768]{3,2,1,0:T(8,128)}) custom-call(bf16[2,128,512]{2,1,0:T(8,128)(2,1)S(1)} %get-tuple-element.4.in_h, f32[3,128,768]{2,1,0:T(8,128)S(1)} %get-tuple-element.5.proj_h), custom_call_target="tpu_custom_call" | custom-call | tf_op jit(solution)/shard_map/pallas_call | solution.py:541

commit v8 on v7

--- a/solution.py
+++ b/solution.py
@@ -26,7 +26,7 @@
     n_dp, n_ex, cap, cp,
     ids_h, probs_h, tok_h, og_h, pre_h, gw_h, uw_h, dw, bs,
     in_out, total,
-    ids, probs, tok, og, tok2, og2, ids2, probs2, idsd, pick_v, sx, sg, rx, rg, dyc, spr, dfull, bfull, gw, uw, pre,
+    ids, probs, tok, og, tok2, og2, ids2, probs2, idsd, pick_v, sx, sg, rx, rg, dyc, spr, dfull, bfull, gw, uw, gwt, uwt, pre,
     act_a, act_b, hid, gu, px, pdy, rs, rr, in_v, psend, prec, term,
     local_sem, pre_sem, dy_s, dy_r, x_s, x_r, mate_s, mate_r, down_s, down_r, base_s, base_r,
     gu_s, gu_r, ret_s, ret_r, px_s, px_r, proj_s, proj_r, in_s, in_r, ids_s, ids_r, ready,
@@ -93,6 +93,22 @@
     for copy in first:
         copy.start()
 
+    barrier = pltpu.get_barrier_semaphore()
+
+    for i in range(1, n_dp):
+        pl.semaphore_signal(barrier, inc=1, device_id={"dp": dp_peer(i)}, device_id_type=MESH)
+
+    odd = lax.rem(me, 2)
+
+    @pl.loop(odd, half)
+    def _(k):
+        hub = lax.rem(me + 1 - odd + 2 * k, n_ex)
+        pl.semaphore_signal(barrier, inc=1, device_id={"expert": hub}, device_id_type=MESH)
+
+    @pl.when(odd == 1)
+    def _():
+        pl.semaphore_signal(barrier, inc=1, device_id={"expert": me - 1}, device_id_type=MESH)
+
     pad = gu.shape[3] - lcap
     if pad:
         for j in range(LEVELS):
@@ -101,22 +117,6 @@
                 px[n_dp - 1 + i, j, lcap:, :] = jnp.zeros((pad, rk), BF16)
                 for s in range(2):
                     gu[i, j, s, lcap:, :] = jnp.zeros((pad, hidden), BF16)
-
-    barrier = pltpu.get_barrier_semaphore()
-
-    for i in range(1, n_dp):
-        pl.semaphore_signal(barrier, inc=1, device_id={"dp": dp_peer(i)}, device_id_type=MESH)
-
-    odd = lax.rem(me, 2)
-
-    @pl.loop(odd, half)
-    def _(k):
-        hub = lax.rem(me + 1 - odd + 2 * k, n_ex)
-        pl.semaphore_signal(barrier, inc=1, device_id={"expert": hub}, device_id_type=MESH)
-
-    @pl.when(odd == 1)
-    def _():
-        pl.semaphore_signal(barrier, inc=1, device_id={"expert": me - 1}, device_id_type=MESH)
 
     local = [
         pltpu.make_async_copy(og_h, og, local_sem.at[0]),
@@ -137,19 +137,19 @@
 
     def down_copy(i, owner, peer):
         return pltpu.make_async_remote_copy(
-            dw.at[0], dfull.at[wpart(owner)], down_s.at[i], down_r.at[i],
+            dw.at[0], dfull.at[wpart(owner)], down_s.at[i - 1], down_r.at[i - 1],
             device_id={"dp": peer}, device_id_type=MESH,
         )
 
     def base_copy(i, owner, peer):
         return pltpu.make_async_remote_copy(
-            bs.at[0], bfull.at[wpart(owner)], base_s.at[i], base_r.at[i],
+            bs.at[0], bfull.at[wpart(owner)], base_s.at[i - 1], base_r.at[i - 1],
             device_id={"dp": peer}, device_id_type=MESH,
         )
 
     def ids_copy(i, peer):
         return pltpu.make_async_remote_copy(
-            ids_h, idsd.at[i - 1], ids_s.at[i], ids_r.at[i],
+            ids_h, idsd.at[i - 1], ids_s.at[i - 1], ids_r.at[i - 1],
             device_id={"dp": peer}, device_id_type=MESH,
         )
 
@@ -181,32 +181,32 @@
 
     def gu_copy(i, j, peer):
         return pltpu.make_async_remote_copy(
-            gu.at[0, j, :, used], gu.at[i, j, :, used], gu_s.at[i, j], gu_r.at[i, j],
+            gu.at[0, j, :, used], gu.at[i, j, :, used], gu_s.at[i - 1, j], gu_r.at[i - 1, j],
             device_id={"dp": peer}, device_id_type=MESH,
         )
 
     def px_copy(i, peer):
         return pltpu.make_async_remote_copy(
-            px.at[i - 1, :, used], px.at[n_dp - 1 + i, :, used], px_s.at[i], px_r.at[i],
-            device_id={"dp": peer}, device_id_type=MESH,
-        )
-
-    def ret_copy(i, j, peer, owner):
-        return pltpu.make_async_remote_copy(
-            rs.at[i, j, block(lax.rem(peer, nl))], rr.at[i, block(owner)],
+            px.at[i - 1, :, used], px.at[n_dp - 1 + i, :, used], px_s.at[i - 1], px_r.at[i - 1],
+            device_id={"dp": peer}, device_id_type=MESH,
+        )
+
+    def ret_copy(i, j, peer, owner, cols):
+        return pltpu.make_async_remote_copy(
+            rs.at[i, j, block(lax.rem(peer, nl)), cols], rr.at[i, block(owner), cols],
             ret_s.at[i], ret_r.at[i],
             device_id={"expert": peer}, device_id_type=MESH,
         )
 
     def proj_copy(i, peer):
         return pltpu.make_async_remote_copy(
-            psend.at[i - 1], prec.at[i - 1], proj_s.at[i], proj_r.at[i],
+            psend.at[i - 1], prec.at[i - 1], proj_s.at[i - 1], proj_r.at[i - 1],
             device_id={"dp": peer}, device_id_type=MESH,
         )
 
     def in_copy(i, owner, peer):
         return pltpu.make_async_remote_copy(
-            in_v.at[i - 1], in_out.at[owner], in_s.at[i], in_r.at[i],
+            in_v.at[i - 1], in_out.at[owner], in_s.at[i - 1], in_r.at[i - 1],
             device_id={"dp": peer}, device_id_type=MESH,
         )
 
@@ -305,16 +305,26 @@
             hid[j, :, cols] = (gs * u).astype(BF16)
             act_b[j, :, cols] = u * sig * (1.0 + g * (1.0 - sig))
 
-    def row_grad(i, j):
-        out = dot(gu[i, j, 0], gw[...], NT) + dot(gu[i, j, 1], uw[...], NT)
-        rs[i, j] = dot(spr[...], out.astype(BF16), TN).astype(BF16)
-
-        @pl.loop(int(j == own), nl)
-        def _(t):
-            ret_copy(i, j, in_level(j, t), me).start()
+    def row_grad(i, j, pieces=1):
+        span = part // pieces
+        for piece in range(pieces):
+            cols = pl.ds(piece * span, span)
+            out = dot(gu[i, j, 0], gwt[:, cols], NN) + dot(gu[i, j, 1], uwt[:, cols], NN)
+            rs[i, j, :, cols] = dot(spr[...], out.astype(BF16), TN).astype(BF16)
+
+            @pl.loop(int(j == own), nl)
+            def _(t):
+                ret_copy(i, j, in_level(j, t), me, cols).start()
 
         if j == own:
             rr[i, block(me), :] = rs[i, j, block(spot), :]
+
+    same = lax.broadcasted_iota(jnp.int32, (fw, fw), 0) == lax.broadcasted_iota(jnp.int32, (fw, fw), 1)
+    same = jnp.where(same, one, zero).astype(BF16)
+    for copy, weights, turned in ((local[4], gw, gwt), (local[5], uw, uwt)):
+        copy.wait()
+        for f in range(0, hidden, fw):
+            turned[f : f + fw, :] = dot(same, weights[:, f : f + fw], NT).astype(BF16)
 
     pick_v[0] = pick_of(ids, 0, rows)[0]
     for i in range(1, n_dp):
@@ -348,9 +358,6 @@
             gu[0, j, 0, :, cols] = (hg * act_b[j, :, cols]).astype(BF16)
         for i in range(1, n_dp):
             gu_copy(i, j, dp_peer(i)).start()
-        if j == 0:
-            local[4].wait()
-            local[5].wait()
         row_grad(0, j)
 
     local[3].wait()
@@ -376,7 +383,7 @@
             gu_copy(i, j, dp_peer(i)).wait_recv()
             if j == own and i == n_dp - 1:
                 pl.when(odd == 0)(start_projections)
-            row_grad(i, j)
+            row_grad(i, j, 2 if j == own and part % 256 == 0 else 1)
 
     theirs(0)
 
@@ -503,6 +510,8 @@
         pltpu.VMEM((width, rank), BF16),
         pltpu.VMEM((part, hidden), BF16),
         pltpu.VMEM((part, hidden), BF16),
+        pltpu.VMEM((hidden, part), BF16),
+        pltpu.VMEM((hidden, part), BF16),
         pltpu.VMEM((LEVELS, lpad, hidden2), BF16),
         pltpu.VMEM((LEVELS, lpad, hidden), F32),
         pltpu.VMEM((LEVELS, lpad, hidden), F32),
@@ -518,10 +527,10 @@
         pltpu.VMEM((rank, hidden), F32),
         dma((8,)), dma((LEVELS,)),
         dma((2,)), dma((LEVELS,)), dma((2,)), dma((1,)), dma((4,)), dma((4,)),
-        dma((n_dp,)), dma((n_dp,)), dma((n_dp,)), dma((n_dp,)),
-        dma((n_dp, LEVELS)), dma((n_dp, LEVELS)), dma((n_dp,)), dma((n_dp,)),
-        dma((n_dp,)), dma((n_dp,)), dma((n_dp,)), dma((n_dp,)),
-        dma((n_dp,)), dma((n_dp,)), dma((n_dp,)), dma((n_dp,)),
+        dma((n_dp - 1,)), dma((n_dp - 1,)), dma((n_dp - 1,)), dma((n_dp - 1,)),
+        dma((n_dp - 1, LEVELS)), dma((n_dp - 1, LEVELS)), dma((n_dp,)), dma((n_dp,)),
+        dma((n_dp - 1,)), dma((n_dp - 1,)), dma((n_dp - 1,)), dma((n_dp - 1,)),
+        dma((n_dp - 1,)), dma((n_dp - 1,)), dma((n_dp - 1,)), dma((n_dp - 1,)),
         pltpu.SemaphoreType.REGULAR,
     ]
     outputs = tok_rows * width * 2 + 3 * rk * hidden * 4

time: 72 us -> 71.7 us (level)
  no operation moved by 1% of the time
where the time goes in v8:
time: 71.7 us; the launch traced here: 71.6 us
  Pallas kernels  70.9 us (99%)
    pallas_call x1, Pallas kernels, body(): pl.pallas_call(functools.partial(kernel, n_dp, n_ex, cap, cp), out_shape=...  69.8 us

profile of v8, /device:TPU:0, one launch (start us, length us, event | category | flops | bytes accessed | tf_op | source)
XLA Modules:
  0.0 71.6 jit_solution(2511316115334026570)
XLA Ops:
  0.6 69.8 %shard_map.104 = (bf16[2,128,512]{2,1,0:T(8,128)(2,1)S(1)}, f32[3,128,768]{2,1,0:T(8,128)S(1)}) custom-call(s32[3,128]{1,0:T(4,128)} %bitcast.2, f32[3,128]{1,0:T(4,128)} %bitcast.3, bf16[128,1024]{1,0:T(8,128)(2,1)} %tok_h.1, bf16[128,1024]{1,0:T(8,128)(2,1)} %og_h.1, bf16[1,1,480,1536]{3,2,1,0:T(8,128)(2,1)} %pre_h.1, bf16[1,512,768]{2,1,0:T(8,128)(2,1)} %gw_h.1, ...), custom_call_target="tpu_custom_call" | custom-call | tf_op jit(solution)/shard_map/pallas_call | solution.py:537
  70.4 1.1 %shard_map.105 = (bf16[128,1024]{1,0:T(8,128)(2,1)}, f32[1,3,128,768]{3,2,1,0:T(8,128)}) custom-call(bf16[2,128,512]{2,1,0:T(8,128)(2,1)S(1)} %get-tuple-element.4.in_h, f32[3,128,768]{2,1,0:T(8,128)S(1)} %get-tuple-element.5.proj_h), custom_call_target="tpu_custom_call" | custom-call | tf_op jit(solution)/shard_map/pallas_call | solution.py:550

commit v9 on v8

--- a/solution.py
+++ b/solution.py
@@ -191,10 +191,26 @@
             device_id={"dp": peer}, device_id_type=MESH,
         )
 
-    def ret_copy(i, j, peer, owner, cols):
+    halves = 2 if part % 256 == 0 else 1
+
+    def cut(i):
+        return halves if i else 1
+
+    def piece_cols(i, piece):
+        return pl.ds(piece * (part // cut(i)), part // cut(i))
+
+    def ret_all(i, piece):
+        span = rr.at[i, pl.ds(0, (n_ex - 1) * cp), piece_cols(i, piece)]
+        return pltpu.make_async_remote_copy(
+            span, span, ret_s.at[i, piece], ret_r.at[i, piece],
+            device_id={"expert": mate}, device_id_type=MESH,
+        )
+
+    def ret_copy(i, j, peer, owner, piece):
+        cols = piece_cols(i, piece)
         return pltpu.make_async_remote_copy(
             rs.at[i, j, block(lax.rem(peer, nl)), cols], rr.at[i, block(owner), cols],
-            ret_s.at[i], ret_r.at[i],
+            ret_s.at[i, piece], ret_r.at[i, piece],
             device_id={"expert": peer}, device_id_type=MESH,
         )
 
@@ -204,9 +220,11 @@
             device_id={"dp": peer}, device_id_type=MESH,
         )
 
-    def in_copy(i, owner, peer):
-        return pltpu.make_async_remote_copy(
-            in_v.at[i - 1], in_out.at[owner], in_s.at[i - 1], in_r.at[i - 1],
+    def in_copy(i, piece, owner, peer):
+        cols = piece_cols(i, piece)
+        return pltpu.make_async_remote_copy(
+            in_v.at[i - 1, :, cols], in_out.at[owner, :, cols],
+            in_s.at[i - 1, piece], in_r.at[i - 1, piece],
             device_id={"dp": peer}, device_id_type=MESH,
         )
 
@@ -305,16 +323,15 @@
             hid[j, :, cols] = (gs * u).astype(BF16)
             act_b[j, :, cols] = u * sig * (1.0 + g * (1.0 - sig))
 
-    def row_grad(i, j, pieces=1):
-        span = part // pieces
-        for piece in range(pieces):
-            cols = pl.ds(piece * span, span)
+    def row_grad(i, j):
+        for piece in range(cut(i)):
+            cols = piece_cols(i, piece)
             out = dot(gu[i, j, 0], gwt[:, cols], NN) + dot(gu[i, j, 1], uwt[:, cols], NN)
             rs[i, j, :, cols] = dot(spr[...], out.astype(BF16), TN).astype(BF16)
 
             @pl.loop(int(j == own), nl)
             def _(t):
-                ret_copy(i, j, in_level(j, t), me, cols).start()
+                ret_copy(i, j, in_level(j, t), me, piece).start()
 
         if j == own:
             rr[i, block(me), :] = rs[i, j, block(spot), :]
@@ -383,7 +400,7 @@
             gu_copy(i, j, dp_peer(i)).wait_recv()
             if j == own and i == n_dp - 1:
                 pl.when(odd == 0)(start_projections)
-            row_grad(i, j, 2 if j == own and part % 256 == 0 else 1)
+            row_grad(i, j)
 
     theirs(0)
 
@@ -417,16 +434,17 @@
     for s in range(2):
         total[s] = x_term(s, 0)
 
-    def combine(i):
-        blocks(rr.at[i], n_ex - 1, ret_s.at[i], ret_r.at[i]).wait_recv()
-        return dot(pick_v[i], rr[i], TN).astype(BF16)
-
-    in_out[my_dp] = combine(0)
+    def combine(i, piece):
+        ret_all(i, piece).wait_recv()
+        return dot(pick_v[i], rr[i, :, piece_cols(i, piece)], TN).astype(BF16)
+
+    in_out[my_dp] = combine(0, 0)
 
     theirs(3)
     for i in range(1, n_dp):
-        in_v[i - 1] = combine(i)
-        in_copy(i, my_dp, dp_from(i)).start()
+        for piece in range(cut(i)):
+            in_v[i - 1, :, piece_cols(i, piece)] = combine(i, piece)
+            in_copy(i, piece, my_dp, dp_from(i)).start()
 
     for i in range(1, n_dp):
         proj_copy(i, dp_peer(i)).wait_recv()
@@ -450,10 +468,12 @@
         blocks(rg, half - 1, dy_s.at[m], dy_r.at[0]).wait_send()
         blocks(rx, half - 1, x_s.at[m], x_r.at[0]).wait_send()
     for i in range(n_dp):
-        blocks(rr.at[i], n_ex - 1, ret_s.at[i], ret_r.at[i]).wait_send()
-    for i in range(1, n_dp):
-        in_copy(i, my_dp, dp_from(i)).wait_send()
-        in_copy(i, dp_peer(i), dp_from(i)).wait_recv()
+        for piece in range(cut(i)):
+            ret_all(i, piece).wait_send()
+    for i in range(1, n_dp):
+        for piece in range(cut(i)):
+            in_copy(i, piece, my_dp, dp_from(i)).wait_send()
+            in_copy(i, piece, dp_peer(i), dp_from(i)).wait_recv()
 
 
 def finish(in_h, proj_h, in_ref, proj_ref, proj_s, in_s):
@@ -528,9 +548,9 @@
         dma((8,)), dma((LEVELS,)),
         dma((2,)), dma((LEVELS,)), dma((2,)), dma((1,)), dma((4,)), dma((4,)),
         dma((n_dp - 1,)), dma((n_dp - 1,)), dma((n_dp - 1,)), dma((n_dp - 1,)),
-        dma((n_dp - 1, LEVELS)), dma((n_dp - 1, LEVELS)), dma((n_dp,)), dma((n_dp,)),
+        dma((n_dp - 1, LEVELS)), dma((n_dp - 1, LEVELS)), dma((n_dp, 2)), dma((n_dp, 2)),
         dma((n_dp - 1,)), dma((n_dp - 1,)), dma((n_dp - 1,)), dma((n_dp - 1,)),
-        dma((n_dp - 1,)), dma((n_dp - 1,)), dma((n_dp - 1,)), dma((n_dp - 1,)),
+        dma((n_dp - 1, 2)), dma((n_dp - 1, 2)), dma((n_dp - 1,)), dma((n_dp - 1,)),
         pltpu.SemaphoreType.REGULAR,
     ]
     outputs = tok_rows * width * 2 + 3 * rk * hidden * 4

time: 71.7 us -> 71.2 us (level)
  no operation moved by 1% of the time
where the time goes in v9:
time: 71.2 us; the launch traced here: 71 us
  Pallas kernels  70.4 us (99%)
    pallas_call x1, Pallas kernels, body(): pl.pallas_call(functools.partial(kernel, n_dp, n_ex, cap, cp), out_shape=...  69.2 us

profile of v9, /device:TPU:0, one launch (start us, length us, event | category | flops | bytes accessed | tf_op | source)
XLA Modules:
  0.0 71.0 jit_solution(12486417420456833029)
XLA Ops:
  0.6 69.2 %shard_map.104 = (bf16[2,128,512]{2,1,0:T(8,128)(2,1)S(1)}, f32[3,128,768]{2,1,0:T(8,128)S(1)}) custom-call(s32[3,128]{1,0:T(4,128)} %bitcast.2, f32[3,128]{1,0:T(4,128)} %bitcast.3, bf16[128,1024]{1,0:T(8,128)(2,1)} %tok_h.1, bf16[128,1024]{1,0:T(8,128)(2,1)} %og_h.1, bf16[1,1,480,1536]{3,2,1,0:T(8,128)(2,1)} %pre_h.1, bf16[1,512,768]{2,1,0:T(8,128)(2,1)} %gw_h.1, ...), custom_call_target="tpu_custom_call" | custom-call | tf_op jit(solution)/shard_map/pallas_call | solution.py:557
  69.9 1.1 %shard_map.105 = (bf16[128,1024]{1,0:T(8,128)(2,1)}, f32[1,3,128,768]{3,2,1,0:T(8,128)}) custom-call(bf16[2,128,512]{2,1,0:T(8,128)(2,1)S(1)} %get-tuple-element.4.in_h, f32[3,128,768]{2,1,0:T(8,128)S(1)} %get-tuple-element.5.proj_h), custom_call_target="tpu_custom_call" | custom-call | tf_op jit(solution)/shard_map/pallas_call | solution.py:570
